TPU v7x, 32 devices: a whole 2x2x4 slice. The times are simulated.
32 devices in a mesh: slab: 4 (over y, core), bl: 8 (over z, x).
Axes of the slice: x: 2, y: 2, z: 4, core: 2. Of those that a mesh axis runs over, the one named last changes fastest.
Arguments:
- model_image: float32 [2, 8192, 8192], P(None, 'slab', 'bl'), may hold values from -6 to 6
- vis_coords: float32 [512, 2, 128], P(('slab', 'bl')), may hold values from 0 to 32
- vis_observed: float32 [512, 2, 128], P(('slab', 'bl')), may hold values from -6 to 6
- tile_slot: int32 [512], P(('slab', 'bl')), may hold values from 0 to 2047
- tile_group: int32 [512, 1], P(('slab', 'bl')), may hold values from 0 to 7; in each aligned block of 16 rows (0 to 15, 16 to 31, ...) at most 8 rows name the same one
- w_plane: int32 [512], P(('slab', 'bl')), may hold values from 0 to 7
- vis_count: int32 [512], P(('slab', 'bl')), may hold values from 16 to 128, as said below
Outputs:
- residual_image: float32 [2, 8192, 8192], P(None, 'slab', 'bl')
- residual_vis: float32 [512, 2, 128], P(('slab', 'bl'))
Inputs may be any that keep to these rules, and one draw needn't show every extreme that they name: `tile_group`: among the 16 subgrids of one device, at most 8 name the same group. `vis_count`: some subgrid holds exactly 128 visibilities.
All inputs are finite; a program needn't handle non-finite values.
Results may differ from a plain program's by a relative error of at most 0.0003.
Values sent between devices are 32-bit elements; how exact they have to be, the bound alone decides.
A program may use at most 192 MiB of HBM per device.

v0:
```python
import math

import jax
import jax.numpy as jnp
from jax import lax
from jax.sharding import PartitionSpec as P

N = 8192
SUB = 32


w_step = 0.1


def complex_einsum(form, left, right):
    product = lambda first, second: jnp.einsum(form, first, second, precision=lax.Precision.HIGHEST)
    return (
        product(left[0], right[0]) - product(left[1], right[1]),
        product(left[0], right[1]) + product(left[1], right[0]),
    )


def complex_mul(left, right):
    return (left[0] * right[0] - left[1] * right[1], left[0] * right[1] + left[1] * right[0])


def subgrid_pass(tile_real, tile_imag, coords, observed, planes, counts):
    width = tile_real.shape[-1]
    half = width // 2
    slots = coords.shape[-1]
    index = jnp.arange(width, dtype=jnp.int32)
    offsets = (index - half).astype(jnp.float32)
    turns = index[:, None] * (index[None, :] - half) % width
    angle = 2.0 * math.pi / width * turns.astype(jnp.float32)
    forward_d = (jnp.cos(angle), jnp.sin(angle))
    backward_d = (forward_d[0], -forward_d[1])
    scale_sub = 1.0 / (width * width)
    halfway = complex_einsum("il,kij->klj", forward_d, (tile_real, tile_imag))
    image_sub = complex_einsum("klj,jm->klm", halfway, forward_d)
    image_sub = (image_sub[0] * scale_sub, image_sub[1] * scale_sub)
    radius = (offsets[:, None] ** 2 + offsets[None, :] ** 2) / (half * half)
    phase = -w_step * planes.astype(jnp.float32)[:, None, None] * radius[None]
    screen = (jnp.cos(phase), jnp.sin(phase))
    weighted = complex_mul(screen, image_sub)
    along_a = -2.0 * math.pi / width * coords[:, 0, :][:, None, :] * offsets[None, :, None]
    along_b = -2.0 * math.pi / width * coords[:, 1, :][:, None, :] * offsets[None, :, None]
    phase_a = (jnp.cos(along_a), jnp.sin(along_a))
    phase_b = (jnp.cos(along_b), jnp.sin(along_b))
    partial_rows = complex_einsum("klm,kmj->klj", weighted, phase_b)
    terms = complex_mul(phase_a, partial_rows)
    predicted = (jnp.sum(terms[0], axis=1), jnp.sum(terms[1], axis=1))
    live = (jnp.arange(slots, dtype=jnp.int32)[None, :] < counts[:, None]).astype(jnp.float32)
    resid_real = (observed[:, 0, :] - predicted[0]) * live
    resid_imag = (observed[:, 1, :] - predicted[1]) * live
    spread = complex_mul(
        (phase_a[0], -phase_a[1]), (resid_real[:, None, :], resid_imag[:, None, :])
    )
    collected = complex_einsum("klj,kmj->klm", spread, (phase_b[0], -phase_b[1]))
    unscreened = complex_mul((screen[0], -screen[1]), collected)
    middle = complex_einsum("il,klm->kim", backward_d, unscreened)
    tile_out = complex_einsum("kim,jm->kij", middle, backward_d)
    return (
        jnp.stack([resid_real, resid_imag], axis=1),
        jnp.stack([tile_out[0] * scale_sub, tile_out[1] * scale_sub], axis=1),
    )


def run_blocks(tile_stack, coords, observed, planes, counts):
    total = tile_stack.shape[0]
    slots = coords.shape[-1]
    width = tile_stack.shape[-1]
    block_size = math.gcd(total, 64)
    block_count = total // block_size

    def one_block(pieces):
        block_tiles, block_coords, block_obs, block_planes, block_counts = pieces
        return subgrid_pass(
            block_tiles[:, 0],
            block_tiles[:, 1],
            block_coords,
            block_obs,
            block_planes,
            block_counts,
        )

    resid_vis, contrib = lax.map(
        one_block,
        (
            tile_stack.reshape(block_count, block_size, 2, width, width),
            coords.reshape(block_count, block_size, 2, slots),
            observed.reshape(block_count, block_size, 2, slots),
            planes.reshape(block_count, block_size),
            counts.reshape(block_count, block_size),
        ),
    )
    return (resid_vis.reshape(total, 2, slots), contrib.reshape(total, 2 * width * width))


def table(first, second, modulus, turn_sign):
    product = first[:, None] * second[None, :] % modulus
    angle = 2.0 * math.pi / modulus * product.astype(jnp.float32)
    real, imag = jnp.cos(angle), turn_sign * jnp.sin(angle)
    return jnp.stack([jnp.stack([real, imag], 1), jnp.stack([-imag, real], 1)])


def turned(form, left, right):
    return jnp.einsum(form, left, right, precision=lax.Precision.HIGH)


def twiddled(block, twiddle):
    real, imag = block[:, 0], block[:, 1]
    return jnp.stack(complex_mul((real, imag), twiddle), axis=1)


def per_device(model_image, vis_coords, vis_observed, tile_slot, tile_group, w_plane, vis_count):
    groups = lax.axis_size("bl")
    bands = lax.axis_size("slab")
    both = ("slab", "bl")
    spread_rows = lax.all_to_all(model_image, "bl", split_axis=1, concat_axis=2, tiled=True)
    rows, length = spread_rows.shape[1:]
    ntile = length // SUB
    outer, inner = jnp.arange(SUB, dtype=jnp.int32), jnp.arange(ntile, dtype=jnp.int32)
    own_rows = lax.axis_index(both) * rows + jnp.arange(rows, dtype=jnp.int32)
    twiddle = table(outer, inner, length, -1.0)[0]
    twiddle = (twiddle[:, 0], twiddle[:, 1])

    shaped = spread_rows.reshape(2, rows, SUB, ntile)
    halfway = turned("prki,pkqj->rqji", shaped, table(outer, outer, SUB, -1.0))
    halfway = twiddled(halfway, twiddle)
    columns = turned("rpji,piqt->tqjr", halfway, table(inner, inner, ntile, -1.0) / N)
    columns = columns.reshape(ntile, 2 * SUB * rows)

    sub_count = tile_slot.shape[0]
    tile_cols = ntile // (bands * groups)
    band = lax.axis_index("slab")
    own_tv = (band * groups + tile_group[:, 0]) * tile_cols + tile_slot // ntile
    own_tu = tile_slot % ntile
    named = lax.all_gather(jnp.stack([own_tu, own_tv], axis=1), both, tiled=True)
    total = named.shape[0]
    chunk = math.gcd(total, 512)
    named = named.reshape(total // chunk, chunk, 2)
    inside = table(own_rows, outer, length, -1.0)
    outward = table(outer, own_rows, length, 1.0)

    def pick(place):
        return (place[:, None] == inner[None, :]).astype(jnp.float32)

    def row_turn(place):
        angle = 2.0 * math.pi / ntile * (place[:, None] * own_rows[None, :] % ntile).astype(jnp.float32)
        return jnp.cos(angle)[:, None, :], jnp.sin(angle)[:, None, :]

    def gather_tiles(ids):
        got = turned("gt,tx->gx", pick(ids[:, 1]), columns).reshape(chunk, 2, SUB, rows)
        real, imag = row_turn(ids[:, 0])
        got = twiddled(got, (real, -imag))
        return turned("gpjr,prqi->gqij", got, inside).reshape(chunk, 2 * SUB * SUB)

    partial = lax.map(gather_tiles, named).reshape(total, 2 * SUB * SUB)
    mine = lax.psum_scatter(partial, both, scatter_dimension=0, tiled=True)
    mine = mine.reshape(sub_count, 2, SUB, SUB)
    residual_vis, contrib = run_blocks(mine, vis_coords, vis_observed, w_plane, vis_count)
    everyone = lax.all_gather(contrib, both, tiled=True)

    def spread_tiles(ids, tiles):
        made = turned("gpij,piqr->gqjr", tiles.reshape(chunk, 2, SUB, SUB), outward)
        made = twiddled(made, row_turn(ids[:, 0])).reshape(chunk, 2 * SUB * rows)
        return turned("gt,gx->tx", pick(ids[:, 1]), made)

    everyone = everyone.reshape(total // chunk, chunk, 2 * SUB * SUB)
    summed = spread_tiles(named[0], everyone[0])
    if total > chunk:
        summed, _ = lax.scan(
            lambda acc, piece: (acc + spread_tiles(*piece), None), summed, (named[1:], everyone[1:])
        )
    summed = summed.reshape(ntile, 2, SUB, rows)
    halfway = turned("tpjr,ptqi->rqji", summed, table(inner, inner, ntile, 1.0))
    halfway = twiddled(halfway, (twiddle[0], -twiddle[1]))
    image = turned("rpji,pjqk->qrki", halfway, table(outer, outer, SUB, 1.0) / N)
    residual_image = lax.all_to_all(
        image.reshape(2, rows, length), "bl", split_axis=2, concat_axis=1, tiled=True
    )
    return (residual_image, residual_vis)


def solution(mesh):
    placed = (
        P(None, "slab", "bl"),
        P(("slab", "bl"), None, None),
        P(("slab", "bl"), None, None),
        P(("slab", "bl")),
        P(("slab", "bl"), None),
        P(("slab", "bl")),
        P(("slab", "bl")),
    )
    return jax.shard_map(
        per_device,
        mesh=mesh,
        in_specs=placed,
        out_specs=(P(None, "slab", "bl"), P(("slab", "bl"), None, None)),
        check_vma=False,
    )
```

profile of v0, /device:TPU:0, one launch (start us, length us, event | category | flops | bytes accessed | tf_op | source)
XLA Modules:
  0.0 1445.9 jit_solution(13843325933783445740)
XLA Ops:
  7.2 28.6 %copy.110 = f32[2,2048,1024]{2,0,1:T(2,128)} copy(f32[2,2048,1024]{2,1,0:T(8,128)} %param.7) | data formatting | bytes 33554432 | tf_op args[0]
  35.8 7.4 all-to-all-start
  43.3 418.1 %all-gather = s32[32,16,2]{1,2,0:T(2,128)S(1)} all-gather(s32[1,16,2]{1,2,0:T(2,128)S(1)} %add_bitcast_fusion), channel_id=1, replica_groups=mesh['slab'=4,'bl'=8] {'slab','bl'}, dimensions={0}, use_global_device_ids=true | all-gather | bytes 4224 | tf_op jit(solution)/shard_map/all_gather | solution.py:138
  462.1 0.6 fusion.150
  462.8 1.0 fusion.143
  463.7 1.0 broadcast_multiply_fusion
  464.7 1.0 fusion.141
  465.8 1.2 fusion.41
  467.0 2.1 fusion.100
  469.1 18.1 %copy.214 = f32[2,8,256,1024]{3,1,0,2:T(8,128)} copy(f32[2,8,256,1024]{3,0,2,1:T(2,128)} %bitcast.34) | data formatting | bytes 33554432 | tf_op jit(solution)/shard_map/all_to_all | solution.py:119
  487.2 19.0 %reshape.733 = f32[2,256,32,256,1]{3,2,0,1,4:T(8,128)} reshape(f32[2,256,8,1024]{3,2,0,1:T(8,128)} %bitcast.235) | data formatting | bytes 33554432 | tf_op jit(solution)/shard_map/reshape | solution.py:127
  506.2 14.3 convolution_bitcast_fusion.1
  520.5 7.2 multiply_subtract_fusion.3
  527.7 6.3 pad_maximum_fusion.1
  534.0 29.6 %fusion.9 = f32[2,256,256,32,1]{1,2,4,3,0:T(8,128)} fusion(f32[256,2,32,256]{3,2,0,1:T(8,128)} %pad_maximum_fusion.1, f32[1,256,2,256]{3,1,0,2:T(8,128)S(1)} %get-tuple-element.60, f32[1,256,2,256]{3,1,0,2:T(8,128)S(1)} %get-tuple-element.61), kind=kOutput, calls=%fused_computation.14 | convolution fusion | flops 12885426176 | bytes 34603008 | tf_op jit(solution)/shard_map/rpji,piqt->tqjr/dot_general | solution.py:107
  563.6 32.2 %fusion.5 = f32[512,2,32,256]{3,0,2,1:T(8,128)} fusion(f32[2,256,256,32,1]{1,2,4,3,0:T(8,128)} %fusion.9, s32[512]{0:T(512)S(1)} %bitcast.256), kind=kOutput, calls=%fused_computation.10 | convolution fusion | flops 12885164032 | bytes 50333696 | tf_op jit(solution)/shard_map/while/body/eval_jaxpr/gt,tx->gx/dot_general | solution.py:107
  595.8 21.9 %multiply_subtract_fusion.1 = (f32[512,1,32,256]{3,0,2,1:T(8,128)}, f32[512,1,32,256]{3,0,2,1:T(8,128)}) fusion(f32[512,2,32,256]{3,0,2,1:T(8,128)} %fusion.5, f32[512,256]{1,0:T(8,128)S(1)} %get-tuple-element.78, f32[512,256]{1,0:T(8,128)S(1)} %get-tuple-element.79), kind=kLoop, calls=%fused_computation.22 | loop fusion | flops 25165824 | bytes 68157440 | tf_op jit(solution)/shard_map/while/body/eval_jaxpr/sub | solution.py:24
  617.7 22.6 %fusion.21 = f32[512,2,32,32]{0,2,3,1:T(8,128)} fusion(f32[1,256,2,32]{1,3,0,2:T(8,128)S(1)} %get-tuple-element.66, f32[1,256,2,32]{1,3,0,2:T(8,128)S(1)} %get-tuple-element.65, f32[512,1,32,256]{3,0,2,1:T(8,128)} %get-tuple-element.44, f32[512,1,32,256]{3,0,2,1:T(8,128)} %get-tuple-element.35), kind=kOutput, calls=%fused_computation.33 | convolution fusion | flops 3229646848 | bytes 37879808 | tf_op jit(solution)/shard_map/while/body/eval_jaxpr/gpjr,prqi->gqij/dot_general | solution.py:107
  640.4 6.7 copy.115
  647.0 5.4 copy.181
  652.5 0.4 all-gather.3.cloned.1.call-start
  653.1 141.9 %reduce-scatter.4.cloned.1.call-done = f32[16,2048]{1,0:T(8,128)} async-done(((f32[512,2048]{1,0:T(8,128)}), f32[16,2048]{1,0:T(8,128)}) %reduce-scatter.4.cloned.1.call-update) | async-done | bytes 131088
  795.0 1.2 copy.182
  796.3 0.4 copy.184
  796.7 0.4 copy.183
  797.1 0.4 fusion.94
  797.6 0.4 fusion.98
  798.0 0.4 fusion.33
  798.4 0.6 fusion.195
  799.0 0.6 fusion.181
  799.6 0.4 fusion.32
  800.1 0.6 fusion.31
  800.7 0.6 fusion.30
  801.3 2.3 fusion.54
  803.6 2.2 fusion.52
  805.8 2.3 convolution_subtract_fusion.3
  808.1 3.5 fusion.83
  811.7 2.4 fusion.51
  814.1 2.4 fusion.73
  816.5 2.4 convolution_subtract_fusion.2
  818.9 2.4 convolution_add_fusion.2
  821.3 1.6 fusion.187
  822.9 1.8 fusion.191
  824.7 1.6 fusion.29
  826.3 0.6 fusion.189
  826.9 0.6 fusion.176
  827.5 1.6 fusion.28
  829.2 0.6 fusion.27
  829.8 0.6 fusion.25
  830.5 0.9 reshape.727
  831.7 58.3 %all-gather.3.cloned.1.call-done = f32[512,2048]{1,0:T(8,128)} async-done(((f32[16,2048]{1,0:T(8,128)}), f32[512,2048]{1,0:T(8,128)}) %all-gather.3.cloned.1.call-update) | async-done | bytes 4194320 | tf_op jit(solution)/shard_map/all_gather | solution.py:162
  890.1 5.3 copy.132
  895.4 21.9 %convolution_bitcast_fusion = f32[512,2,32,256]{3,0,2,1:T(8,128)} fusion(f32[512,2,32,32]{0,3,2,1:T(8,128)} %bitcast.236, f32[1,32,2,256]{3,1,0,2:T(8,128)S(1)} %get-tuple-element.64, f32[1,32,2,256]{3,1,0,2:T(8,128)S(1)} %get-tuple-element.63), kind=kOutput, calls=%fused_computation.7 | convolution fusion | flops 3221258240 | bytes 37879808 | tf_op jit(solution)/shard_map/gpij,piqr->gqjr/dot_general | solution.py:107
  917.3 22.3 %multiply_subtract_fusion = (f32[512,1,32,256]{3,0,2,1:T(8,128)}, f32[512,1,32,256]{3,0,2,1:T(8,128)}) fusion(f32[512,2,32,256]{3,0,2,1:T(8,128)} %convolution_bitcast_fusion, f32[512,256]{1,0:T(8,128)S(1)} %get-tuple-element.77, f32[512,256]{1,0:T(8,128)S(1)} %get-tuple-element.79), kind=kLoop, calls=%fused_computation.20 | loop fusion | flops 25165824 | bytes 68157440 | tf_op jit(solution)/shard_map/sub | solution.py:24
  939.7 21.8 %fusion.13 = f32[256,2,32,256,1]{3,0,1,2,4:T(8,128)} fusion(s32[512]{0:T(512)S(1)} %bitcast.257, f32[512,1,32,256]{3,0,2,1:T(8,128)} %get-tuple-element.34, f32[512,1,32,256]{3,0,2,1:T(8,128)} %get-tuple-element.33), kind=kOutput, calls=%fused_computation.23 | convolution fusion | flops 12893421568 | bytes 50333696 | tf_op jit(solution)/shard_map/gt,gx->tx/dot_general | solution.py:107
  961.4 20.3 %copy.165 = f32[256,2,32,256,1]{0,2,1,3,4:T(8,128)} copy(f32[256,2,32,256,1]{3,0,1,2,4:T(8,128)} %fusion.13) | data formatting | bytes 33554432 | tf_op jit(solution)/shard_map/gt,gx->tx/dot_general | solution.py:107
  981.7 20.1 %convolution_bitcast_fusion.2 = f32[256,2,32,256]{3,2,0,1:T(8,128)} fusion(f32[256,2,32,256,1]{0,2,1,3,4:T(8,128)} %copy.165, f32[1,256,2,256]{3,1,2,0:T(8,128)S(1)} %copy-done.1, f32[1,256,2,256]{3,1,2,0:T(8,128)S(1)} %copy-done), kind=kOutput, calls=%fused_computation.30 | convolution fusion | flops 12885164032 | bytes 34603008 | tf_op jit(solution)/shard_map/tpjr,ptqi->rqji/dot_general | solution.py:107
  1001.8 9.8 multiply_subtract_fusion.2
  1011.6 13.3 fusion.16
  1025.0 19.6 %copy.180 = f32[2,256,32,256]{1,0,3,2:T(2,128)} copy(f32[2,256,32,256]{3,2,1,0:T(8,128)} %fusion.16) | data formatting | bytes 33554432 | tf_op jit(solution)/shard_map/reshape | solution.py:180
  1044.6 5.8 all-to-all-start.1
  1050.4 0.6 pad_maximum_fusion.12
  1051.0 362.9 %all-to-all-done.1 = f32[2,256,8192]{1,0,2:T(2,128)} async-done(((f32[2,256,8192]{1,0,2:T(2,128)}), f32[2,256,8192]{1,0,2:T(2,128)}, u32[]{:S(2)}, u32[]{:S(2)}) %all-to-all-start.1) | async-done | bytes 16777248 | tf_op jit(solution)/shard_map/all_to_all | solution.py:179
  1413.9 24.9 %copy.142 = f32[2,8,256,1024]{3,2,1,0:T(8,128)} copy(f32[2,8,256,1024]{2,0,3,1:T(2,128)} %bitcast.89) | data formatting | bytes 33554432 | tf_op jit(solution)/shard_map/all_to_all | solution.py:179
  (53 shorter events, 1.5 us)
Async XLA Ops:
  35.8 7.5 copy-start.9
  35.8 7.5 copy-start.10
  35.8 433.3 %all-to-all-start = ((f32[2,2048,1024]{2,0,1:T(2,128)}), f32[2,2048,1024]{2,0,1:T(2,128)}, u32[]{:S(2)}, u32[]{:S(2)}) async-start(f32[2,2048,1024]{2,0,1:T(2,128)} %copy.110), calls=%async_computation | async-start | bytes 33554432 | tf_op jit(solution)/shard_map/all_to_all | solution.py:119
  43.2 751.8 %reduce-scatter.4.cloned.1.call-start = ((), (), s32[]{:S(2)}) async-start(), calls=%async_computation.4 | async-start | bytes 4325376
  462.0 58.6 %copy-start.2 = (f32[32,256]{1,0:T(8,128)}, f32[32,256]{1,0:T(8,128)S(1)}, u32[]{:S(2)}) copy-start(f32[32,256]{1,0:T(8,128)S(1)} %get-tuple-element.93) | copy-start | bytes 98308
  640.4 12.6 copy-start.11
  640.4 12.7 copy-start.7
  640.4 171.2 %copy-start.6 = (f32[16,2,128]{2,1,0:T(2,128)S(1)}, f32[16,2,128]{2,1,0:T(2,128)}, u32[]{:S(2)}) copy-start(f32[16,2,128]{2,1,0:T(2,128)} %param.9) | copy-start | bytes 49156
  640.4 171.2 %copy-start.8 = (s32[16]{0:T(128)S(1)}, s32[16]{0:T(128)}, u32[]{:S(2)}) copy-start(s32[16]{0:T(128)} %param.13) | copy-start | bytes 196
  652.5 237.6 %all-gather.3.cloned.1.call-start = ((), (), s32[]{:S(2)}) async-start(), calls=%async_computation.3 | async-start | bytes 4325376 | tf_op jit(solution)/shard_map/all_gather | solution.py:162
  961.4 20.3 %copy-start = (f32[1,256,2,256]{3,1,2,0:T(8,128)S(1)}, f32[1,256,2,256]{3,1,2,0:T(8,128)}, u32[]{:S(2)}) copy-start(f32[1,256,2,256]{3,1,2,0:T(8,128)} %get-tuple-element.51) | copy-start | bytes 1572868
  961.4 20.3 %copy-start.1 = (f32[1,256,2,256]{3,1,2,0:T(8,128)S(1)}, f32[1,256,2,256]{3,1,2,0:T(8,128)}, u32[]{:S(2)}) copy-start(f32[1,256,2,256]{3,1,2,0:T(8,128)} %get-tuple-element.62) | copy-start | bytes 1572868
  981.7 20.1 %copy-start.3 = (f32[32,256]{1,0:T(8,128)S(1)}, f32[32,256]{1,0:T(8,128)}, u32[]{:S(2)}) copy-start(f32[32,256]{1,0:T(8,128)} %copy-done.2) | copy-start | bytes 98308
  1001.8 9.8 copy-start.4
  1001.8 9.8 copy-start.5
  1044.6 369.3 %all-to-all-start.1 = ((f32[2,256,8192]{1,0,2:T(2,128)}), f32[2,256,8192]{1,0,2:T(2,128)}, u32[]{:S(2)}, u32[]{:S(2)}) async-start(f32[2,256,8192]{1,0,2:T(2,128)} %bitcast.234), calls=%async_computation.1 | async-start | bytes 33554432 | tf_op jit(solution)/shard_map/all_to_all | solution.py:179
Sparse Core Ops, SparseCore 0:
  652.6 142.3 reduce-scatter.3
  831.5 58.4 all-gather.2
where the time goes:
time: 1450 us
  waiting for transfers between devices  563 us (39%)
  blocking collectives  418 us (29%)
  matrix products  209 us (14%)
  local copies, waits for them, and re-layouts  151 us (10%)
  other arithmetic  76.2 us (5%)
  between operations  14.6 us (1%)
    all_gather x1, blocking collectives, per_device(): lax.all_gather(jnp.stack([own_tu, own_tv], axis=1), both, tiled=True)  418 us
    all_to_all x1, waiting for transfers between devices, per_device(): lax.all_to_all(image.reshape(2, rows, length), 'bl', split_axis=2, concat...  363 us
    dot_general x8, matrix products, turned(): return jnp.einsum(form, left, right, precision=lax.Precision.HIGH)  176 us
    unnamed x3, waiting for transfers between devices  142 us
    sub x4, other arithmetic, complex_mul(): left[0] * right[0] - left[1] * right[1]  61.2 us
    all_gather x1, waiting for transfers between devices, per_device(): everyone = lax.all_gather(contrib, both, tiled=True)  58.3 us
    unnamed x30, local copies, waits for them, and re-layouts  36.1 us
    dot_general x24, matrix products, complex_einsum(): jnp.einsum(form, first, second, precision=lax.Precision.HIGHEST)  33 us
  transfers between devices with their start and end apart: 4, of which 3 were waited for; matrix products, arithmetic and copies ran while one was open for 1% of the time, Pallas kernels for 0%

commit v1 on v0

v1 whole, which is shorter than its diff:
```python
import functools
import math

import jax
import jax.numpy as jnp
import numpy as np
from jax import lax
from jax.experimental import pallas as pl
from jax.experimental.pallas import tpu as pltpu
from jax.sharding import PartitionSpec as P

SUB = 32
LANES = 128
F32, BF16 = jnp.float32, jnp.bfloat16

w_step = 0.1


def complex_einsum(form, left, right):
    product = lambda first, second: jnp.einsum(form, first, second, precision=lax.Precision.HIGHEST)
    return (
        product(left[0], right[0]) - product(left[1], right[1]),
        product(left[0], right[1]) + product(left[1], right[0]),
    )


def complex_mul(left, right):
    return (left[0] * right[0] - left[1] * right[1], left[0] * right[1] + left[1] * right[0])


def subgrid_pass(tile_real, tile_imag, coords, observed, planes, counts):
    width = tile_real.shape[-1]
    half = width // 2
    slots = coords.shape[-1]
    index = jnp.arange(width, dtype=jnp.int32)
    offsets = (index - half).astype(jnp.float32)
    turns = index[:, None] * (index[None, :] - half) % width
    angle = 2.0 * math.pi / width * turns.astype(jnp.float32)
    forward_d = (jnp.cos(angle), jnp.sin(angle))
    backward_d = (forward_d[0], -forward_d[1])
    scale_sub = 1.0 / (width * width)
    halfway = complex_einsum("il,kij->klj", forward_d, (tile_real, tile_imag))
    image_sub = complex_einsum("klj,jm->klm", halfway, forward_d)
    image_sub = (image_sub[0] * scale_sub, image_sub[1] * scale_sub)
    radius = (offsets[:, None] ** 2 + offsets[None, :] ** 2) / (half * half)
    phase = -w_step * planes.astype(jnp.float32)[:, None, None] * radius[None]
    screen = (jnp.cos(phase), jnp.sin(phase))
    weighted = complex_mul(screen, image_sub)
    along_a = -2.0 * math.pi / width * coords[:, 0, :][:, None, :] * offsets[None, :, None]
    along_b = -2.0 * math.pi / width * coords[:, 1, :][:, None, :] * offsets[None, :, None]
    phase_a = (jnp.cos(along_a), jnp.sin(along_a))
    phase_b = (jnp.cos(along_b), jnp.sin(along_b))
    partial_rows = complex_einsum("klm,kmj->klj", weighted, phase_b)
    terms = complex_mul(phase_a, partial_rows)
    predicted = (jnp.sum(terms[0], axis=1), jnp.sum(terms[1], axis=1))
    live = (jnp.arange(slots, dtype=jnp.int32)[None, :] < counts[:, None]).astype(jnp.float32)
    resid_real = (observed[:, 0, :] - predicted[0]) * live
    resid_imag = (observed[:, 1, :] - predicted[1]) * live
    spread = complex_mul(
        (phase_a[0], -phase_a[1]), (resid_real[:, None, :], resid_imag[:, None, :])
    )
    collected = complex_einsum("klj,kmj->klm", spread, (phase_b[0], -phase_b[1]))
    unscreened = complex_mul((screen[0], -screen[1]), collected)
    middle = complex_einsum("il,klm->kim", backward_d, unscreened)
    tile_out = complex_einsum("kim,jm->kij", middle, backward_d)
    return (
        jnp.stack([resid_real, resid_imag], axis=1),
        jnp.stack([tile_out[0] * scale_sub, tile_out[1] * scale_sub], axis=1),
    )


def turn(value, modulus):
    angle = 2.0 * math.pi / modulus * (value % modulus).astype(F32)
    return jnp.cos(angle), jnp.sin(angle)


def split(value):
    high = lax.reduce_precision(value, 8, 7)
    return high.astype(BF16), (value - high).astype(BF16)


def split_in(value):
    high = value.astype(BF16)
    return high, (value - high.astype(F32)).astype(BF16)


def times_unit(pair, numerator, denominator):
    re, im = pair
    eighth = 8 * numerator % (8 * denominator)
    if eighth % denominator == 0:
        eighth //= denominator
        r = math.sqrt(0.5)
        if eighth == 0:
            return re, im
        if eighth == 2:
            return -im, re
        if eighth == 4:
            return -re, -im
        if eighth == 6:
            return im, -re
        if eighth == 1:
            return (re - im) * r, (re + im) * r
        if eighth == 3:
            return (re + im) * -r, (re - im) * r
        if eighth == 5:
            return (im - re) * r, (re + im) * -r
        return (re + im) * r, (im - re) * r
    angle = 2.0 * math.pi * (numerator % denominator) / denominator
    c, s = math.cos(angle), math.sin(angle)
    return re * c - im * s, re * s + im * c


def small_fft(values, sign):
    n = len(values)
    if n == 1:
        return values
    even, odd = small_fft(values[0::2], sign), small_fft(values[1::2], sign)
    out = [None] * n
    for k in range(n // 2):
        re, im = times_unit(odd[k], sign * k, n)
        out[k] = (even[k][0] + re, even[k][1] + im)
        out[k + n // 2] = (even[k][0] - re, even[k][1] - im)
    return out


def forward_kernel(
    tu_ref, image_ref, other_ref, dft2_ref, dft1_ref, turn_ref, col_ref, e_ref, out_ref,
    x_buf, z_buf, u_buf, lhs_buf, sems, *, ntile, blocks, chunk,
):
    step = pl.program_id(0)
    core = lax.rem(lax.axis_index("slab"), 2)
    kr = x_buf.shape[2]
    half = kr // 2
    per = SUB // kr
    tiles = ntile // 16

    def copies(block, slot):
        mine = pl.multiple_of(core * (blocks * LANES) + block * LANES, LANES)
        theirs = pl.multiple_of(block * LANES, LANES)
        return (
            pltpu.make_async_copy(
                image_ref.at[:, :, :, pl.ds(mine, LANES)],
                x_buf.at[slot, :, pl.ds(core * half, half)], sems.at[slot, 0]),
            pltpu.make_async_copy(
                other_ref.at[:, :, :, pl.ds(theirs, LANES)],
                x_buf.at[slot, :, pl.ds((1 - core) * half, half)], sems.at[slot, 1]),
        )

    @pl.when(step == 0)
    def _():
        for copy in copies(0, 0):
            copy.start()

        def one_block(block, carry):
            slot = lax.rem(block, 2)

            @pl.when(block + 1 < blocks)
            def _():
                for copy in copies(block + 1, 1 - slot):
                    copy.start()

            for copy in copies(block, slot):
                copy.wait()

            def rows(tile, carry):
                at = pl.ds(pl.multiple_of(tile * 16, 16), 16)
                turns = turn_ref[at, :]
                for q in range(per):
                    values = []
                    for k in range(kr):
                        pair = (x_buf[slot, 0, k, at, :], x_buf[slot, 1, k, at, :])
                        values.append(times_unit(pair, -q * k, SUB))
                    for m, (re, im) in enumerate(small_fft(values, -1)):
                        i = per * m + q
                        c = jnp.broadcast_to(turns[:, 2 * i:2 * i + 1], re.shape)
                        s = jnp.broadcast_to(turns[:, 2 * i + 1:2 * i + 2], re.shape)
                        lane = pl.ds(i % 2 * LANES, LANES)
                        for part, value in enumerate((re * c + im * s, im * c - re * s)):
                            high, low = split_in(value)
                            z_buf[i // 2, part, at, lane] = high
                            z_buf[i // 2, part + 2, at, lane] = low
                return carry

            lax.fori_loop(0, tiles, rows, 0)

            def pairs(pair, carry):
                z = z_buf[pair].reshape(4 * ntile, 2 * LANES)
                u = jnp.dot(dft2_ref[...], z, preferred_element_type=F32)
                u += jnp.dot(dft1_ref[...], z[:2 * ntile], preferred_element_type=F32)
                for part in range(2):
                    for side in range(2):
                        plane = pl.multiple_of((part * SUB + pair * 2 + side) * ntile, ntile)
                        u_buf[block, pl.ds(plane, ntile), :] = u[
                            part * ntile:(part + 1) * ntile, side * LANES:(side + 1) * LANES]
                return carry

            lax.fori_loop(0, SUB // 2, pairs, 0)
            return carry

        lax.fori_loop(0, blocks, one_block, 0)

    wide = blocks * LANES

    def one(g, carry):
        tu = tu_ref[step * chunk + g]
        rows = pl.ds(pl.multiple_of(g * SUB, SUB), SUB)
        for block in range(blocks):
            x = u_buf[block, pl.ds(tu, 2 * SUB, ntile), :]
            c, s = e_ref[g, 2 * block:2 * block + 1, :], e_ref[g, 2 * block + 1:2 * block + 2, :]
            re, im = x[:SUB], x[SUB:]
            for part, value in enumerate((re * c + im * s, im * c - re * s)):
                high, low = split_in(value)
                lhs_buf[rows, pl.ds(part * wide + block * LANES, LANES)] = high
                lhs_buf[rows, pl.ds((part + 2) * wide + block * LANES, LANES)] = low
        return carry

    lax.fori_loop(0, chunk, one, 0, unroll=2)
    made = jnp.dot(lhs_buf[...], col_ref[...], preferred_element_type=F32)
    made = made + pltpu.roll(made, LANES // 2, 1)
    made = made.reshape(chunk, SUB, LANES)
    left = lax.broadcasted_iota(jnp.int32, (chunk, SUB // 2, LANES), 2) < LANES // 2
    out_ref[...] = jnp.where(left, made[:, :SUB // 2], made[:, SUB // 2:])


def backward_kernel(
    tu_ref, c_ref, dft2_ref, dft1_ref, turn_ref, col_ref, e_ref, image_ref, other_ref,
    x_buf, y_buf, s_buf, p_buf, sems, *, ntile, blocks, chunk, steps,
):
    step = pl.program_id(0)
    core = lax.rem(lax.axis_index("slab"), 2)
    kr = x_buf.shape[2]
    half = kr // 2
    per = SUB // kr
    wide = blocks * LANES

    @pl.when(step == 0)
    def _():
        zero = jnp.zeros((ntile, LANES), F32)

        def clear(plane, carry):
            for block in range(blocks):
                s_buf[block, pl.ds(pl.multiple_of(plane * ntile, ntile), ntile), :] = zero
            return carry

        lax.fori_loop(0, 2 * SUB, clear, 0)

    given = c_ref[...]
    turned = pltpu.roll(given.reshape(chunk * SUB // 2, LANES), LANES // 2, 1).reshape(given.shape)
    left = lax.broadcasted_iota(jnp.int32, given.shape, 2) < LANES // 2
    both = jnp.concatenate([jnp.where(left, given, turned), jnp.where(left, turned, given)], axis=1)
    high, low = split_in(both.reshape(chunk * SUB, LANES))
    p_buf[...] = jnp.dot(jnp.concatenate([high, low], axis=1), col_ref[...], preferred_element_type=F32)

    def one(g, carry):
        tu = tu_ref[step * chunk + g]
        rows = pl.ds(pl.multiple_of(g * SUB, SUB), SUB)
        for block in range(blocks):
            re = p_buf[rows, pl.ds(block * LANES, LANES)]
            im = p_buf[rows, pl.ds(wide + block * LANES, LANES)]
            c, s = e_ref[g, 2 * block:2 * block + 1, :], e_ref[g, 2 * block + 1:2 * block + 2, :]
            at = pl.ds(tu, 2 * SUB, ntile)
            s_buf[block, at, :] = s_buf[block, at, :] + jnp.concatenate(
                [re * c - im * s, re * s + im * c], axis=0)
        return carry

    lax.fori_loop(0, chunk, one, 0, unroll=2)

    def copies(block, slot):
        mine = pl.multiple_of(core * wide + block * LANES, LANES)
        theirs = pl.multiple_of(block * LANES, LANES)
        return (
            pltpu.make_async_copy(
                x_buf.at[slot, :, pl.ds(core * half, half)],
                image_ref.at[:, :, :, pl.ds(mine, LANES)], sems.at[slot, 0]),
            pltpu.make_async_copy(
                x_buf.at[slot, :, pl.ds((1 - core) * half, half)],
                other_ref.at[:, :, :, pl.ds(theirs, LANES)], sems.at[slot, 1]),
        )

    @pl.when(step == steps - 1)
    def _():
        def one_block(block, carry):
            slot = lax.rem(block, 2)

            def pairs(pair, carry):
                parts = []
                for part in range(2):
                    sides = []
                    for side in range(2):
                        plane = pl.multiple_of((part * SUB + pair * 2 + side) * ntile, ntile)
                        sides.append(s_buf[block, pl.ds(plane, ntile), :])
                    parts.append(jnp.concatenate(sides, axis=1))
                high, low = split_in(jnp.concatenate(parts, axis=0))
                y = jnp.dot(dft2_ref[...], jnp.concatenate([high, low], axis=0), preferred_element_type=F32)
                y += jnp.dot(dft1_ref[...], high, preferred_element_type=F32)
                for part in range(2):
                    for side in range(2):
                        y_buf[pair * 2 + side, part] = y[
                            part * ntile:(part + 1) * ntile, side * LANES:(side + 1) * LANES]
                return carry

            lax.fori_loop(0, SUB // 2, pairs, 0)

            @pl.when(block >= 2)
            def _():
                for copy in copies(block - 2, slot):
                    copy.wait()

            def rows(tile, carry):
                at = pl.ds(pl.multiple_of(tile * 8, 8), 8)
                turns = turn_ref[at, :]
                total = [None] * kr
                for q in range(per):
                    values = []
                    for m in range(kr):
                        i = per * m + q
                        re, im = y_buf[i, 0, at, :], y_buf[i, 1, at, :]
                        c = jnp.broadcast_to(turns[:, 2 * i:2 * i + 1], re.shape)
                        s = jnp.broadcast_to(turns[:, 2 * i + 1:2 * i + 2], re.shape)
                        values.append((re * c - im * s, re * s + im * c))
                    for k, value in enumerate(small_fft(values, 1)):
                        re, im = times_unit(value, q * k, SUB)
                        total[k] = (re, im) if q == 0 else (total[k][0] + re, total[k][1] + im)
                for k in range(kr):
                    x_buf[slot, 0, k, at, :] = total[k][0]
                    x_buf[slot, 1, k, at, :] = total[k][1]
                return carry

            lax.fori_loop(0, ntile // 8, rows, 0)
            for copy in copies(block, slot):
                copy.start()
            return carry

        lax.fori_loop(0, blocks, one_block, 0)
        for block in range(max(0, blocks - 2), blocks):
            for copy in copies(block, block % 2):
                copy.wait()


def complex_table(cos, sin):
    return jnp.concatenate(
        [jnp.concatenate([cos, -sin], axis=1), jnp.concatenate([sin, cos], axis=1)], axis=0)


def per_device(model_image, vis_coords, vis_observed, tile_slot, tile_group, w_plane, vis_count):
    groups = lax.axis_size("bl")
    bands = lax.axis_size("slab")
    both = ("slab", "bl")
    rows, cols = model_image.shape[1:]
    length = rows * bands
    ntile = length // SUB
    band = lax.axis_index("slab")
    core = lax.rem(band, 2)
    wide = cols // 2
    blocks = wide // LANES
    kr = 2 * rows // ntile
    swap = [(d, d ^ 1) for d in range(bands)]

    leaving = lax.dynamic_slice_in_dim(model_image, (1 - core) * wide, wide, axis=2)
    other = lax.ppermute(leaving, "slab", swap)

    sub_count = tile_slot.shape[0]
    tile_cols = ntile // (bands * groups)
    own_tv = (band * groups + tile_group[:, 0]) * tile_cols + tile_slot // ntile
    own_tu = tile_slot % ntile
    named = lax.all_gather(jnp.stack([own_tu, own_tv], axis=0), both, axis=1, tiled=True)
    tu, tv = named[0], named[1]
    total = tu.shape[0]
    chunk = math.gcd(total, 16)
    steps = total // chunk

    inner = jnp.arange(ntile, dtype=jnp.int32)
    outer = jnp.arange(SUB, dtype=jnp.int32)
    own_cols = lax.axis_index("bl") * cols + core * wide + jnp.arange(wide, dtype=jnp.int32)
    first_row = band // 2 * (2 * rows)

    dft_c, dft_s = turn(inner[:, None] * inner[None, :], ntile)
    fwd_high, fwd_low = split(complex_table(dft_c, -dft_s))
    bwd_high, bwd_low = split(complex_table(dft_c, dft_s))
    turns = jnp.stack(turn((first_row + inner)[:, None] * outer[None, :], length), axis=2)
    turns = jnp.pad(turns.reshape(ntile, 2 * SUB), ((0, 0), (0, LANES - 2 * SUB)))
    col_c, col_s = turn(own_cols[:, None] * outer[None, :], length)
    col_c, col_s = col_c / length, col_s / length
    out_high, out_low = split(jnp.concatenate(
        [jnp.concatenate([col_c, -col_s], axis=1), jnp.concatenate([col_s, col_c], axis=1)], axis=0))
    zero = jnp.zeros_like(out_high)
    col_fwd = jnp.concatenate(
        [jnp.concatenate([out_high, out_low], axis=1), jnp.concatenate([out_high, zero], axis=1)], axis=0)
    in_high, in_low = split(jnp.concatenate(
        [jnp.concatenate([col_c.T, col_s.T], axis=1), jnp.concatenate([-col_s.T, col_c.T], axis=1)], axis=0))
    col_bwd = jnp.concatenate([in_high, in_low, in_high, in_low], axis=0)
    e_c, e_s = turn(tv[:, None] * own_cols[None, :], ntile)
    e_table = jnp.stack([e_c.reshape(total, blocks, LANES), e_s.reshape(total, blocks, LANES)], axis=2)
    e_table = e_table.reshape(total, 2 * blocks, LANES)

    whole = lambda shape: pl.BlockSpec(shape, lambda step, ids: (0,) * len(shape))
    by_step = lambda shape: pl.BlockSpec(shape, lambda step, ids: (step,) + (0,) * (len(shape) - 1))
    anywhere = pl.BlockSpec(memory_space=pl.ANY)
    params = pltpu.CompilerParams(
        dimension_semantics=("arbitrary",), vmem_limit_bytes=67_000_000)
    partial = pl.pallas_call(
        functools.partial(forward_kernel, ntile=ntile, blocks=blocks, chunk=chunk),
        grid_spec=pltpu.PrefetchScalarGridSpec(
            num_scalar_prefetch=1,
            grid=(steps,),
            in_specs=[
                anywhere, anywhere,
                whole((2 * ntile, 4 * ntile)), whole((2 * ntile, 2 * ntile)), whole((ntile, LANES)),
                whole((4 * wide, LANES)), by_step((chunk, 2 * blocks, LANES)),
            ],
            out_specs=by_step((chunk, SUB // 2, LANES)),
            scratch_shapes=[
                pltpu.VMEM((2, 2, kr, ntile, LANES), F32),
                pltpu.VMEM((SUB // 2, 4, ntile, 2 * LANES), BF16),
                pltpu.VMEM((blocks, 2 * SUB * ntile, LANES), F32),
                pltpu.VMEM((chunk * SUB, 4 * wide), BF16),
                pltpu.SemaphoreType.DMA((2, 2)),
            ],
        ),
        out_shape=jax.ShapeDtypeStruct((total, SUB // 2, LANES), F32),
        compiler_params=params,
        name="tiles_from_image",
    )(
        tu,
        model_image.reshape(2, kr // 2, ntile, cols), other.reshape(2, kr // 2, ntile, wide),
        jnp.concatenate([fwd_high, fwd_high], axis=1), fwd_low, turns, col_fwd, e_table,
    )
    mine = lax.psum_scatter(partial, both, scatter_dimension=0, tiled=True)
    mine = mine.reshape(sub_count, SUB // 2, 2, 2, SUB).transpose(3, 0, 2, 1, 4)
    mine = mine.reshape(2, sub_count, SUB, SUB)
    residual_vis, contrib = subgrid_pass(
        mine[0], mine[1], vis_coords, vis_observed, w_plane, vis_count)
    contrib = contrib.reshape(sub_count, 2, 2, SUB // 2, SUB).transpose(0, 3, 2, 1, 4)
    everyone = lax.all_gather(contrib.reshape(sub_count, SUB // 2, LANES), both, tiled=True)

    image, leaving = pl.pallas_call(
        functools.partial(backward_kernel, ntile=ntile, blocks=blocks, chunk=chunk, steps=steps),
        grid_spec=pltpu.PrefetchScalarGridSpec(
            num_scalar_prefetch=1,
            grid=(steps,),
            in_specs=[
                by_step((chunk, SUB // 2, LANES)),
                whole((2 * ntile, 4 * ntile)), whole((2 * ntile, 2 * ntile)), whole((ntile, LANES)),
                whole((8 * SUB, 2 * wide)), by_step((chunk, 2 * blocks, LANES)),
            ],
            out_specs=[anywhere, anywhere],
            scratch_shapes=[
                pltpu.VMEM((2, 2, kr, ntile, LANES), F32),
                pltpu.VMEM((SUB, 2, ntile, LANES), F32),
                pltpu.VMEM((blocks, 2 * SUB * ntile, LANES), F32),
                pltpu.VMEM((chunk * SUB, 2 * wide), F32),
                pltpu.SemaphoreType.DMA((2, 2)),
            ],
        ),
        out_shape=[
            jax.ShapeDtypeStruct((2, kr // 2, ntile, cols), F32),
            jax.ShapeDtypeStruct((2, kr // 2, ntile, wide), F32),
        ],
        compiler_params=params,
        name="image_from_tiles",
    )(
        tu, everyone,
        jnp.concatenate([bwd_high, bwd_high], axis=1), bwd_low, turns, col_bwd, e_table,
    )
    arrived = lax.ppermute(leaving.reshape(2, rows, wide), "slab", swap)
    image = lax.dynamic_update_slice_in_dim(
        image.reshape(2, rows, cols), arrived, (1 - core) * wide, axis=2)
    return (image, residual_vis)


def solution(mesh):
    placed = (
        P(None, "slab", "bl"),
        P(("slab", "bl"), None, None),
        P(("slab", "bl"), None, None),
        P(("slab", "bl")),
        P(("slab", "bl"), None),
        P(("slab", "bl")),
        P(("slab", "bl")),
    )
    return jax.shard_map(
        per_device,
        mesh=mesh,
        in_specs=placed,
        out_specs=(P(None, "slab", "bl"), P(("slab", "bl"), None, None)),
        check_vma=False,
    )
```

time: 1450 us -> 765 us (0.53)
  Pallas kernels: 0 us -> 392 us
  waiting for transfers between devices: 563 us -> 210 us
  blocking collectives: 418 us -> 70 us
  matrix products: 209 us -> 33.7 us
  local copies, waits for them, and re-layouts: 151 us -> 20.1 us
  other arithmetic: 76.2 us -> 14.3 us
    pallas_call x0 -> x2, Pallas kernels: none -> 392 us  [the longest x1 226 us: per_device(): pl.pallas_call(functools.partial(backward_kernel, ntile=ntile, blocks=blo...]
    all_to_all x2 -> x0, waiting for transfers between devices: 363 us -> none  [the longest x1 363 us: per_device(): lax.all_to_all(image.reshape(2, rows, length), 'bl', split_axis=2, concat...]
    all_gather x1, blocking collectives: 418 us -> 70 us  [per_device(): lax.all_gather(jnp.stack([own_tu, own_tv], axis=0), both, axis=1, tiled=T...]
    dot_general x8 -> x0, matrix products: 176 us -> none  [turned(): return jnp.einsum(form, left, right, precision=lax.Precision.HIGH)]
    unnamed x3 -> x2, waiting for transfers between devices: 142 us -> 0.03 us
    reduce_scatter x0 -> x1, waiting for transfers between devices: none -> 140 us  [per_device(): mine = lax.psum_scatter(partial, both, scatter_dimension=0, tiled=True)]
    sub x4 -> x0, other arithmetic: 61.2 us -> none  [complex_mul(): left[0] * right[0] - left[1] * right[1]]
    all_to_all x2 -> x0, local copies, waits for them, and re-layouts: 43 us -> none  [the longest x1 24.9 us: per_device(): lax.all_to_all(image.reshape(2, rows, length), 'bl', split_axis=2, concat...]
  transfers between devices with their start and end apart: 4 -> 4, of which waited for: 3 -> 3; matrix products, arithmetic and copies ran while one was open for 1% -> 2% of each run, Pallas kernels for 0% -> 0%
where the time goes in v1:
time: 765 us; the launch traced here: 756 us
  Pallas kernels  392 us (51%)
  waiting for transfers between devices  210 us (27%)
  blocking collectives  70 us (9%)
  matrix products  33.7 us (4%)
  local copies, waits for them, and re-layouts  20.1 us (3%)
  between operations  14.9 us (2%)
  other arithmetic  14.3 us (2%)
    pallas_call x1, Pallas kernels, per_device(): pl.pallas_call(functools.partial(backward_kernel, ntile=ntile, blocks=blo...  226 us
    pallas_call x1, Pallas kernels, per_device(): pl.pallas_call(functools.partial(forward_kernel, ntile=ntile, blocks=bloc...  166 us
    reduce_scatter x1, waiting for transfers between devices, per_device(): mine = lax.psum_scatter(partial, both, scatter_dimension=0, tiled=True)  140 us
    all_gather x1, blocking collectives, per_device(): lax.all_gather(jnp.stack([own_tu, own_tv], axis=0), both, axis=1, tiled=T...  70 us
    all_gather x1, waiting for transfers between devices, per_device(): lax.all_gather(contrib.reshape(sub_count, SUB // 2, LANES), both, tiled=T...  57.1 us
    dot_general x24, matrix products, complex_einsum(): jnp.einsum(form, first, second, precision=lax.Precision.HIGHEST)  33.7 us
  transfers between devices with their start and end apart: 4, of which 3 were waited for; matrix products, arithmetic and copies ran while one was open for 2% of the time, Pallas kernels for 0%

profile of v1, /device:TPU:0, one launch (start us, length us, event | category | flops | bytes accessed | tf_op | source)
XLA Modules:
  0.0 755.9 jit_solution(5523700970952638326)
XLA Ops:
  7.2 0.0 reduce-scatter.2.cloned.1.call-start
  7.2 7.8 %constant_dynamic-slice_fusion = f32[2,2048,512]{2,1,0:T(8,128)} fusion(f32[2,2048,1024]{2,1,0:T(8,128)} %param.7, s32[]{:T(128)S(6)} %select_n.122), kind=kLoop, calls=%fused_computation.248 | loop fusion | bytes 16777220 | tf_op jit(solution)/shard_map/dynamic_slice | solution.py:359
  15.0 0.5 collective-permute-start
  15.5 70.0 %all-gather = s32[32,16,2]{1,2,0:T(2,128)S(1)} all-gather(s32[1,16,2]{1,2,0:T(2,128)S(1)} %add_bitcast_fusion), channel_id=1, replica_groups=mesh['slab'=4,'bl'=8] {'slab','bl'}, dimensions={0}, use_global_device_ids=true | all-gather | bytes 4224 | tf_op jit(solution)/shard_map/all_gather | solution.py:366
  85.6 0.1 reshape.323
  85.7 0.1 fusion.145
  85.8 0.1 copy.67
  86.0 0.1 copy.68
  86.1 0.1 copy.69
  86.2 0.6 fusion.247
  86.8 4.1 fusion.19
  91.0 0.1 pad_maximum_fusion
  91.1 3.0 copy.70
  94.1 0.7 pad.5.turn_ref
  94.7 1.0 fusion.96
  95.7 1.0 fusion.82
  96.8 1.0 fusion.237
  97.8 0.2 fusion.16
  98.0 1.3 fusion.11
  99.3 1.2 pad_maximum_fusion.5.dft2_ref
  100.4 1.0 fusion.17.col_ref
  101.4 166.0 %tiles_from_image.1 = f32[512,16,128]{2,1,0:T(8,128)} custom-call(s32[512]{0:T(512)} %bitcast.120, f32[2,8,256,1024]{3,2,1,0:T(8,128)} %bitcast.94, f32[2,8,256,512]{3,2,1,0:T(8,128)} %bitcast.9.other_ref, bf16[512,1024]{1,0:T(8,128)(2,1)} %pad_maximum_fusion.5.dft2_ref, bf16[512,512]{1,0:T(8,128)(2,1)} %get-tuple-element.9.dft1_ref, ...), custom_call_target="tpu_custom_call" | custom-call | tf_op jit(solution)/shard_map/tiles_from_image/pallas_call | solution.py:401
  267.5 0.2 all-gather.3.cloned.1.call-start
  267.7 0.4 copy-done.6
  268.1 0.1 add_multiply_fusion
  268.2 140.4 %reduce-scatter.2.cloned.1.call-done = f32[16,16,128]{2,1,0:T(8,128)} async-done(((f32[512,16,128]{2,1,0:T(8,128)}), f32[16,16,128]{2,1,0:T(8,128)}) %reduce-scatter.2.cloned.1.call-update) | async-done | bytes 131088 | tf_op jit(solution)/shard_map/reduce_scatter | solution.py:428
  408.6 1.3 reshape.318
  409.9 0.1 copy.106
  410.0 0.6 fusion.140
  410.6 0.6 fusion.136
  411.2 0.6 fusion.7
  411.9 0.6 fusion.123
  412.5 0.6 fusion.138
  413.1 0.6 fusion.6
  413.7 0.6 fusion.4
  414.3 0.6 fusion.5
  414.9 2.3 fusion.23
  417.1 2.2 fusion.21
  419.4 2.3 convolution_subtract_fusion.3
  421.6 3.5 fusion.52
  425.2 0.1 compare_select_fusion.1
  425.3 2.4 fusion.42
  427.7 2.4 fusion.20
  430.1 2.4 convolution_add_fusion.2
  432.4 2.4 convolution_subtract_fusion.2
  434.9 1.6 fusion.129
  436.5 1.9 fusion.133
  438.4 1.6 fusion.3
  440.0 0.6 fusion.118
  440.6 0.6 fusion.131
  441.2 1.6 fusion.2
  442.8 0.6 fusion.1
  443.4 0.6 fusion
  444.1 0.4 copy.88
  444.5 1.1 reshape.319
  445.6 0.3 sine_multiply_fusion.1
  445.9 0.9 pad_maximum_fusion.7.col_ref
  446.8 1.1 pad_maximum_fusion.6.dft2_ref
  447.9 57.1 %all-gather.3.cloned.1.call-done.c_ref = f32[512,16,128]{2,1,0:T(8,128)} async-done(((f32[16,16,128]{2,1,0:T(8,128)}), f32[512,16,128]{2,1,0:T(8,128)}) %all-gather.3.cloned.1.call-update) | async-done | bytes 4194320 | tf_op jit(solution)/shard_map/all_gather | solution.py:434
  505.0 225.8 %image_from_tiles.1 = (f32[2,8,256,1024]{3,2,1,0:T(8,128)}, f32[2,8,256,512]{3,2,1,0:T(8,128)}) custom-call(s32[512]{0:T(512)} %bitcast.121, f32[512,16,128]{2,1,0:T(8,128)} %all-gather.3.cloned.1.call-done.c_ref, bf16[512,1024]{1,0:T(8,128)(2,1)} %pad_maximum_fusion.6.dft2_ref, bf16[512,512]{1,0:T(8,128)(2,1)} %get-tuple-element.8.dft1_ref, ...), custom_call_target="tpu_custom_call" | custom-call | tf_op jit(solution)/shard_map/image_from_tiles/pallas_call | solution.py:436
  730.8 0.3 collective-permute-start.1
  731.1 0.6 pad_maximum_fusion.9
  731.8 12.5 %collective-permute-done.1 = f32[2,2048,512]{2,1,0:T(8,128)S(1)} collective-permute-done((f32[2,2048,512]{2,1,0:T(8,128)}, f32[2,2048,512]{2,1,0:T(8,128)S(1)}, u32[]{:S(2)}, u32[]{:S(2)}) %collective-permute-start.1) | collective-permute-done | bytes 8388640 | tf_op jit(solution)/shard_map/ppermute | solution.py:465
  744.3 4.4 constant_dynamic-update-slice_fusion
  (33 shorter events, 0.3 us)
Async XLA Ops:
  7.2 401.4 %reduce-scatter.2.cloned.1.call-start = ((), (), s32[]{:S(2)}) async-start(), calls=%async_computation.1 | async-start | bytes 4325376 | tf_op jit(solution)/shard_map/reduce_scatter | solution.py:428
  7.2 8.3 %copy-start.4 = (s32[16]{0:T(128)S(1)}, s32[16]{0:T(128)}, u32[]{:S(2)}) copy-start(s32[16]{0:T(128)} %param.10) | copy-start | bytes 196
  7.2 8.3 %copy-start.5 = (s32[16,1]{0,1:T(1,128)S(1)}, s32[16,1]{0,1:T(1,128)}, u32[]{:S(2)}) copy-start(s32[16,1]{0,1:T(1,128)} %param.11) | copy-start | bytes 196
  15.0 86.4 %collective-permute-start = (f32[2,2048,512]{2,1,0:T(8,128)}, f32[2,2048,512]{2,1,0:T(8,128)}, u32[]{:S(2)}, u32[]{:S(2)}) collective-permute-start(f32[2,2048,512]{2,1,0:T(8,128)} %constant_dynamic-slice_fusion), channel_id=1, source_target_pairs={{0,8},{8,0},{16,24},{24,16},{1,9},{9,1},{17,25},{25,17},{2,10},{10... | collective-permute-start | bytes 25165832 | tf_op jit(solution)/shard_map/ppermute | solution.py:360
  267.4 0.7 copy-start.6
  267.5 0.7 copy-start.2
  267.5 237.5 %all-gather.3.cloned.1.call-start = ((), (), s32[]{:S(2)}) async-start(), calls=%async_computation.2 | async-start | bytes 4325376 | tf_op jit(solution)/shard_map/all_gather | solution.py:434
  411.2 13.9 %copy-start.1 = (f32[16,2,128]{2,1,0:T(2,128)S(1)}, f32[16,2,128]{2,1,0:T(2,128)}, u32[]{:S(2)}) copy-start(f32[16,2,128]{2,1,0:T(2,128)} %param.9) | copy-start | bytes 49156
  411.2 13.9 %copy-start.3 = (s32[16]{0:T(128)S(1)}, s32[16]{0:T(128)}, u32[]{:S(2)}) copy-start(s32[16]{0:T(128)} %param.13) | copy-start | bytes 196
  440.0 6.8 copy-start
  730.8 13.4 %collective-permute-start.1 = (f32[2,2048,512]{2,1,0:T(8,128)}, f32[2,2048,512]{2,1,0:T(8,128)S(1)}, u32[]{:S(2)}, u32[]{:S(2)}) collective-permute-start(f32[2,2048,512]{2,1,0:T(8,128)} %bitcast.132), channel_id=1, source_target_pairs={{0,8},{8,0},{16,24},{24,16},{1,9},{9,1},{17,25},{25,17},{2,10},{10... | collective-permute-start | bytes 25165832 | tf_op jit(solution)/shard_map/ppermute | solution.py:465
Sparse Core Ops, SparseCore 0:
  267.6 140.9 reduce-scatter.1
  445.7 59.2 all-gather.2

commit v2 on v1

--- a/solution.py
+++ b/solution.py
@@ -17,7 +17,7 @@
 
 
 def complex_einsum(form, left, right):
-    product = lambda first, second: jnp.einsum(form, first, second, precision=lax.Precision.HIGHEST)
+    product = lambda first, second: jnp.einsum(form, first, second, precision=lax.Precision.HIGH)
     return (
         product(left[0], right[0]) - product(left[1], right[1]),
         product(left[0], right[1]) + product(left[1], right[0]),
@@ -189,9 +189,10 @@
                 u += jnp.dot(dft1_ref[...], z[:2 * ntile], preferred_element_type=F32)
                 for part in range(2):
                     for side in range(2):
-                        plane = pl.multiple_of((part * SUB + pair * 2 + side) * ntile, ntile)
-                        u_buf[block, pl.ds(plane, ntile), :] = u[
-                            part * ntile:(part + 1) * ntile, side * LANES:(side + 1) * LANES]
+                        plane = pl.multiple_of((part * SUB + pair * 2 + side) * 8, 8)
+                        u_buf[block, :, pl.ds(plane, 8), :] = u[
+                            part * ntile:(part + 1) * ntile, side * LANES:(side + 1) * LANES
+                        ].reshape(ntile // 8, 8, LANES)
                 return carry
 
             lax.fori_loop(0, SUB // 2, pairs, 0)
@@ -205,7 +206,7 @@
         tu = tu_ref[step * chunk + g]
         rows = pl.ds(pl.multiple_of(g * SUB, SUB), SUB)
         for block in range(blocks):
-            x = u_buf[block, pl.ds(tu, 2 * SUB, ntile), :]
+            x = u_buf[block, tu // 8, pl.ds(lax.rem(tu, 8), 2 * SUB, 8), :]
             c, s = e_ref[g, 2 * block:2 * block + 1, :], e_ref[g, 2 * block + 1:2 * block + 2, :]
             re, im = x[:SUB], x[SUB:]
             for part, value in enumerate((re * c + im * s, im * c - re * s)):
@@ -214,7 +215,7 @@
                 lhs_buf[rows, pl.ds((part + 2) * wide + block * LANES, LANES)] = low
         return carry
 
-    lax.fori_loop(0, chunk, one, 0, unroll=2)
+    lax.fori_loop(0, chunk, one, 0, unroll=4)
     made = jnp.dot(lhs_buf[...], col_ref[...], preferred_element_type=F32)
     made = made + pltpu.roll(made, LANES // 2, 1)
     made = made.reshape(chunk, SUB, LANES)
@@ -235,11 +236,11 @@
 
     @pl.when(step == 0)
     def _():
-        zero = jnp.zeros((ntile, LANES), F32)
+        zero = jnp.zeros((ntile // 8, 8, LANES), F32)
 
         def clear(plane, carry):
             for block in range(blocks):
-                s_buf[block, pl.ds(pl.multiple_of(plane * ntile, ntile), ntile), :] = zero
+                s_buf[block, :, pl.ds(pl.multiple_of(plane * 8, 8), 8), :] = zero
             return carry
 
         lax.fori_loop(0, 2 * SUB, clear, 0)
@@ -258,12 +259,12 @@
             re = p_buf[rows, pl.ds(block * LANES, LANES)]
             im = p_buf[rows, pl.ds(wide + block * LANES, LANES)]
             c, s = e_ref[g, 2 * block:2 * block + 1, :], e_ref[g, 2 * block + 1:2 * block + 2, :]
-            at = pl.ds(tu, 2 * SUB, ntile)
-            s_buf[block, at, :] = s_buf[block, at, :] + jnp.concatenate(
+            at = pl.ds(lax.rem(tu, 8), 2 * SUB, 8)
+            s_buf[block, tu // 8, at, :] = s_buf[block, tu // 8, at, :] + jnp.concatenate(
                 [re * c - im * s, re * s + im * c], axis=0)
         return carry
 
-    lax.fori_loop(0, chunk, one, 0, unroll=2)
+    lax.fori_loop(0, chunk, one, 0, unroll=4)
 
     def copies(block, slot):
         mine = pl.multiple_of(core * wide + block * LANES, LANES)
@@ -287,8 +288,8 @@
                 for part in range(2):
                     sides = []
                     for side in range(2):
-                        plane = pl.multiple_of((part * SUB + pair * 2 + side) * ntile, ntile)
-                        sides.append(s_buf[block, pl.ds(plane, ntile), :])
+                        plane = pl.multiple_of((part * SUB + pair * 2 + side) * 8, 8)
+                        sides.append(s_buf[block, :, pl.ds(plane, 8), :].reshape(ntile, LANES))
                     parts.append(jnp.concatenate(sides, axis=1))
                 high, low = split_in(jnp.concatenate(parts, axis=0))
                 y = jnp.dot(dft2_ref[...], jnp.concatenate([high, low], axis=0), preferred_element_type=F32)
@@ -337,6 +338,296 @@
                 copy.wait()
 
 
+MESH = pl.DeviceIdType.MESH
+
+
+def greet(peers):
+    barrier = pltpu.get_barrier_semaphore()
+    for peer in peers:
+        pl.semaphore_signal(barrier, inc=1, device_id=peer, device_id_type=MESH)
+    pl.semaphore_wait(barrier, len(peers))
+
+
+def swap_kernel(ids_ref, image_ref, other_ref, all_ref, send_sem, recv_sem, id_send, id_recv, *, bands, groups):
+    slab, bl = lax.axis_index("slab"), lax.axis_index("bl")
+    core = lax.rem(slab, 2)
+    count = bands * groups
+    me = slab * groups + bl
+    wide = other_ref.shape[-1]
+    barrier = pltpu.get_barrier_semaphore()
+
+    def peer(offset):
+        to = lax.rem(me + offset, count)
+        return (to // groups, lax.rem(to, groups))
+
+    def hello(offset, carry):
+        pl.semaphore_signal(barrier, inc=1, device_id=peer(offset), device_id_type=MESH)
+        return carry
+
+    lax.fori_loop(1, count, hello, 0)
+    pl.semaphore_wait(barrier, count - 1)
+
+    partner = (slab + 1 - 2 * core, bl)
+    away = pl.multiple_of((1 - core) * wide, LANES)
+    swaps = []
+    for part in range(image_ref.shape[0]):
+        for k in range(image_ref.shape[1]):
+            swaps.append(pltpu.make_async_remote_copy(
+                src_ref=image_ref.at[part, k, :, pl.ds(away, wide)],
+                dst_ref=other_ref.at[part, k],
+                send_sem=send_sem.at[part, k], recv_sem=recv_sem.at[part, k],
+                device_id=partner, device_id_type=MESH))
+
+    def tell(offset):
+        return pltpu.make_async_remote_copy(
+            src_ref=ids_ref, dst_ref=all_ref.at[me],
+            send_sem=id_send.at[offset], recv_sem=id_recv.at[offset],
+            device_id=peer(offset), device_id_type=MESH)
+
+    def start(offset, carry):
+        tell(offset).start()
+        return carry
+
+    def finish(offset, carry):
+        tell(offset).wait()
+        return carry
+
+    for swap in swaps:
+        swap.start()
+    lax.fori_loop(1, count, start, 0)
+    all_ref[me] = ids_ref[...]
+    lax.fori_loop(1, count, finish, 0)
+    for swap in swaps:
+        swap.wait()
+
+
+class Grid:
+    def __init__(self, sizes):
+        self.sizes = sizes
+        self.slab, self.bl = lax.axis_index("slab"), lax.axis_index("bl")
+        self.y, self.core = self.slab // 2, lax.rem(self.slab, 2)
+        self.z, self.x = self.bl // sizes["x"], lax.rem(self.bl, sizes["x"])
+
+    def along(self, axis, offset):
+        if axis == "core":
+            return (self.slab + 1 - 2 * self.core, self.bl)
+        at = lax.rem(getattr(self, axis) + offset, self.sizes[axis])
+        if axis == "y":
+            return (at * 2 + self.core, self.bl)
+        if axis == "z":
+            return (self.slab, at * self.sizes["x"] + self.x)
+        return (self.slab, self.z * self.sizes["x"] + at)
+
+    def others(self):
+        peers = [self.along("core", 1)]
+        for axis in "yzx":
+            peers += [self.along(axis, offset) for offset in range(1, self.sizes[axis])]
+        return peers
+
+
+def send(src, dst, sems, at, to):
+    copy = pltpu.make_async_remote_copy(
+        src_ref=src, dst_ref=dst, send_sem=sems.at[(0,) + at], recv_sem=sems.at[(1,) + at],
+        device_id=to, device_id_type=MESH)
+    copy.start()
+    return copy
+
+
+def reduce_kernel(
+    part_ref, out_ref, r0, c0, r1a, c1a, r1b, c1b, r2a, r2b, c2, r3,
+    s_own, s0, s1a, s1b, s2a, s2b, s3, *, sizes,
+):
+    place = Grid(sizes)
+    ny, nz, nx = sizes["y"], sizes["z"], sizes["x"]
+    x, y, z, core = place.x, place.y, place.z, place.core
+    greet(place.others())
+    owns, first = [], []
+    for h in range(2):
+        first.append(send(part_ref.at[:, 1 - core, :, :, h], r0.at[h], s0, (h,), place.along("core", 1)))
+    for h in range(2):
+        own = pltpu.make_async_copy(part_ref.at[:, core, :, :, h], c0.at[h], s_own.at[h])
+        own.start()
+        owns.append(own)
+
+    def total(h):
+        owns[h].wait()
+        first[h].wait_recv()
+
+        def add(at, carry):
+            iy, iz, ix = at // (nz * nx), lax.rem(at // nx, nz), lax.rem(at, nx)
+            c0[h, iy, iz, ix] = c0[h, iy, iz, ix] + r0[h, iy, iz, ix]
+            return carry
+
+        lax.fori_loop(0, ny * nz * nx, add, 0)
+
+    def summed(value, got, *at):
+        for o in range(got.shape[0]):
+            value = value + got[(o,) + at]
+        return value
+
+    total(0)
+    one_a = [send(c0.at[0, lax.rem(y + o, ny)], r1a.at[o - 1], s1a, (o - 1,), place.along("y", o))
+             for o in range(1, ny)]
+    total(1)
+    one_b = [send(c0.at[1, :, :, lax.rem(x + o, nx)], r1b.at[o - 1], s1b, (o - 1,), place.along("x", o))
+             for o in range(1, nx)]
+    for copy in one_a:
+        copy.wait_recv()
+
+    def add_one_a(at, carry):
+        iz, ix = at // nx, lax.rem(at, nx)
+        c1a[iz, ix] = summed(c0[0, y, iz, ix], r1a, iz, ix)
+        return carry
+
+    lax.fori_loop(0, nz * nx, add_one_a, 0)
+    two_a = [send(c1a.at[:, lax.rem(x + o, nx)], r2a.at[o - 1], s2a, (o - 1,), place.along("x", o))
+             for o in range(1, nx)]
+    for copy in one_b:
+        copy.wait_recv()
+
+    def add_one_b(at, carry):
+        iy, iz = at // nz, lax.rem(at, nz)
+        c1b[iy, iz] = summed(c0[1, iy, iz, x], r1b, iy, iz)
+        return carry
+
+    lax.fori_loop(0, ny * nz, add_one_b, 0)
+    two_b = [send(c1b.at[lax.rem(y + o, ny)], r2b.at[o - 1], s2b, (o - 1,), place.along("y", o))
+             for o in range(1, ny)]
+    three = []
+    for h, copies in enumerate((two_a, two_b)):
+        for copy in copies:
+            copy.wait_recv()
+
+        def add_two(iz, carry):
+            c2[h, iz] = summed(c1a[iz, x], r2a, iz) if h == 0 else summed(c1b[y, iz], r2b, iz)
+            return carry
+
+        lax.fori_loop(0, nz, add_two, 0)
+        three.append([
+            send(c2.at[h, lax.rem(z + o, nz)], r3.at[h, o - 1], s3, (h, o - 1), place.along("z", o))
+            for o in range(1, nz)])
+    for h in range(2):
+        for copy in three[h]:
+            copy.wait_recv()
+        value = c2[h, z]
+        for o in range(nz - 1):
+            value = value + r3[h, o]
+        out_ref[h] = value
+    for copy in first + one_a + one_b + two_a + two_b + three[0] + three[1]:
+        copy.wait_send()
+
+
+def gather_kernel(mine_ref, out_ref, s_own, s_z, s_two, s_three, s_core, *, sizes):
+    place = Grid(sizes)
+    x, y, z, core = place.x, place.y, place.z, place.core
+    greet(place.others())
+    own = pltpu.make_async_copy(mine_ref, out_ref.at[y, core, z, x], s_own)
+    own.start()
+    along_z = [
+        [send(mine_ref.at[h], out_ref.at[y, core, z, x, h], s_z, (h, o - 1), place.along("z", o))
+         for o in range(1, sizes["z"])] for h in range(2)]
+    own.wait()
+    two = []
+    for h, axis in enumerate("xy"):
+        for copy in along_z[h]:
+            copy.wait_recv()
+        ref = out_ref.at[y, core, :, x, h]
+        two.append([send(ref, ref, s_two, (h, o - 1), place.along(axis, o)) for o in range(1, sizes[axis])])
+    three = []
+    for h, axis in enumerate("yx"):
+        for copy in two[h]:
+            copy.wait_recv()
+        ref = out_ref.at[y, core, :, :, 0] if h == 0 else out_ref.at[:, core, :, x, 1]
+        three.append([send(ref, ref, s_three, (h, o - 1), place.along(axis, o)) for o in range(1, sizes[axis])])
+    last = []
+    for h in range(2):
+        for copy in three[h]:
+            copy.wait_recv()
+        ref = out_ref.at[:, core, :, :, h]
+        last.append(send(ref, ref, s_core, (h,), place.along("core", 1)))
+    for copy in last:
+        copy.wait_recv()
+    for copy in along_z[0] + along_z[1] + two[0] + two[1] + three[0] + three[1] + last:
+        copy.wait_send()
+
+
+def talk(number):
+    return pltpu.CompilerParams(collective_id=number, has_side_effects=True, vmem_limit_bytes=67_000_000)
+
+
+def swap_and_name(image, ids, bands, groups):
+    halves, wide = image.shape[:3], image.shape[3] // 2
+    count = bands * groups
+    return pl.pallas_call(
+        functools.partial(swap_kernel, bands=bands, groups=groups),
+        in_specs=[pl.BlockSpec(memory_space=pltpu.VMEM), pl.BlockSpec(memory_space=pl.ANY)],
+        out_specs=[pl.BlockSpec(memory_space=pl.ANY), pl.BlockSpec(memory_space=pltpu.VMEM)],
+        out_shape=[
+            jax.ShapeDtypeStruct(halves + (wide,), F32),
+            jax.ShapeDtypeStruct((count,) + ids.shape, jnp.int32),
+        ],
+        scratch_shapes=[
+            pltpu.SemaphoreType.DMA(halves[:2]), pltpu.SemaphoreType.DMA(halves[:2]),
+            pltpu.SemaphoreType.DMA((count,)), pltpu.SemaphoreType.DMA((count,)),
+        ],
+        compiler_params=talk(1),
+        name="swap_columns",
+    )(ids, image)
+
+
+def grid_sizes(bands, groups):
+    ny = bands // 2
+    nx = math.gcd(groups, ny)
+    return {"y": ny, "x": nx, "z": groups // nx}
+
+
+def reduce_tiles(partial, bands, groups):
+    sizes = grid_sizes(bands, groups)
+    ny, nz, nx = sizes["y"], sizes["z"], sizes["x"]
+    total, rows = partial.shape[:2]
+    block = (total // (bands * groups) // 2 * rows, LANES)
+    vmem = lambda *shape: pltpu.VMEM(shape + block, F32)
+    sems = lambda *shape: pltpu.SemaphoreType.DMA((2,) + tuple(max(1, n) for n in shape))
+    out = pl.pallas_call(
+        functools.partial(reduce_kernel, sizes=sizes),
+        in_specs=[pl.BlockSpec(memory_space=pl.ANY)],
+        out_specs=pl.BlockSpec(memory_space=pltpu.VMEM),
+        out_shape=jax.ShapeDtypeStruct((2,) + block, F32),
+        scratch_shapes=[
+            vmem(2, ny, nz, nx), vmem(2, ny, nz, nx),
+            vmem(ny - 1, nz, nx), vmem(nz, nx),
+            vmem(nx - 1, ny, nz), vmem(ny, nz),
+            vmem(nx - 1, nz), vmem(ny - 1, nz), vmem(2, nz), vmem(2, nz - 1),
+            pltpu.SemaphoreType.DMA((2,)), sems(2), sems(ny - 1), sems(nx - 1),
+            sems(nx - 1), sems(ny - 1), sems(2, nz - 1),
+        ],
+        compiler_params=talk(2),
+        name="reduce_tiles",
+    )(partial.reshape((ny, 2, nz, nx, 2) + block))
+    return out.reshape(total // (bands * groups), rows, LANES)
+
+
+def gather_tiles(mine, bands, groups):
+    sizes = grid_sizes(bands, groups)
+    ny, nz, nx = sizes["y"], sizes["z"], sizes["x"]
+    count, rows = mine.shape[:2]
+    block = (count // 2 * rows, LANES)
+    most = max(nx, ny) - 1
+    sems = lambda *shape: pltpu.SemaphoreType.DMA((2,) + shape)
+    out = pl.pallas_call(
+        functools.partial(gather_kernel, sizes=sizes),
+        in_specs=[pl.BlockSpec(memory_space=pltpu.VMEM)],
+        out_specs=pl.BlockSpec(memory_space=pl.ANY),
+        out_shape=jax.ShapeDtypeStruct((ny, 2, nz, nx, 2) + block, F32),
+        scratch_shapes=[
+            pltpu.SemaphoreType.DMA, sems(2, nz - 1), sems(2, most), sems(2, most), sems(2),
+        ],
+        compiler_params=talk(3),
+        name="gather_tiles",
+    )(mine.reshape((2,) + block))
+    return out.reshape(bands * groups * count, rows, LANES)
+
+
 def complex_table(cos, sin):
     return jnp.concatenate(
         [jnp.concatenate([cos, -sin], axis=1), jnp.concatenate([sin, cos], axis=1)], axis=0)
@@ -345,7 +636,6 @@
 def per_device(model_image, vis_coords, vis_observed, tile_slot, tile_group, w_plane, vis_count):
     groups = lax.axis_size("bl")
     bands = lax.axis_size("slab")
-    both = ("slab", "bl")
     rows, cols = model_image.shape[1:]
     length = rows * bands
     ntile = length // SUB
@@ -356,17 +646,17 @@
     kr = 2 * rows // ntile
     swap = [(d, d ^ 1) for d in range(bands)]
 
-    leaving = lax.dynamic_slice_in_dim(model_image, (1 - core) * wide, wide, axis=2)
-    other = lax.ppermute(leaving, "slab", swap)
-
     sub_count = tile_slot.shape[0]
     tile_cols = ntile // (bands * groups)
     own_tv = (band * groups + tile_group[:, 0]) * tile_cols + tile_slot // ntile
     own_tu = tile_slot % ntile
-    named = lax.all_gather(jnp.stack([own_tu, own_tv], axis=0), both, axis=1, tiled=True)
-    tu, tv = named[0], named[1]
+    ids = jnp.pad(jnp.stack([own_tu, own_tv]), ((0, 6), (0, LANES - sub_count)))
+    shaped = model_image.reshape(2, kr // 2, ntile, cols)
+    other, named = swap_and_name(shaped, ids, bands, groups)
+    tu = named[:, 0, :sub_count].reshape(-1)
+    tv = named[:, 1, :sub_count].reshape(-1)
     total = tu.shape[0]
-    chunk = math.gcd(total, 16)
+    chunk = math.gcd(total, 32)
     steps = total // chunk
 
     inner = jnp.arange(ntile, dtype=jnp.int32)
@@ -412,7 +702,7 @@
             scratch_shapes=[
                 pltpu.VMEM((2, 2, kr, ntile, LANES), F32),
                 pltpu.VMEM((SUB // 2, 4, ntile, 2 * LANES), BF16),
-                pltpu.VMEM((blocks, 2 * SUB * ntile, LANES), F32),
+                pltpu.VMEM((blocks, ntile // 8, 2 * SUB * 8, LANES), F32),
                 pltpu.VMEM((chunk * SUB, 4 * wide), BF16),
                 pltpu.SemaphoreType.DMA((2, 2)),
             ],
@@ -422,16 +712,16 @@
         name="tiles_from_image",
     )(
         tu,
-        model_image.reshape(2, kr // 2, ntile, cols), other.reshape(2, kr // 2, ntile, wide),
+        shaped, other,
         jnp.concatenate([fwd_high, fwd_high], axis=1), fwd_low, turns, col_fwd, e_table,
     )
-    mine = lax.psum_scatter(partial, both, scatter_dimension=0, tiled=True)
+    mine = reduce_tiles(partial, bands, groups)
     mine = mine.reshape(sub_count, SUB // 2, 2, 2, SUB).transpose(3, 0, 2, 1, 4)
     mine = mine.reshape(2, sub_count, SUB, SUB)
     residual_vis, contrib = subgrid_pass(
         mine[0], mine[1], vis_coords, vis_observed, w_plane, vis_count)
     contrib = contrib.reshape(sub_count, 2, 2, SUB // 2, SUB).transpose(0, 3, 2, 1, 4)
-    everyone = lax.all_gather(contrib.reshape(sub_count, SUB // 2, LANES), both, tiled=True)
+    everyone = gather_tiles(contrib.reshape(sub_count, SUB // 2, LANES), bands, groups)
 
     image, leaving = pl.pallas_call(
         functools.partial(backward_kernel, ntile=ntile, blocks=blocks, chunk=chunk, steps=steps),
@@ -447,7 +737,7 @@
             scratch_shapes=[
                 pltpu.VMEM((2, 2, kr, ntile, LANES), F32),
                 pltpu.VMEM((SUB, 2, ntile, LANES), F32),
-                pltpu.VMEM((blocks, 2 * SUB * ntile, LANES), F32),
+                pltpu.VMEM((blocks, ntile // 8, 2 * SUB * 8, LANES), F32),
                 pltpu.VMEM((chunk * SUB, 2 * wide), F32),
                 pltpu.SemaphoreType.DMA((2, 2)),
             ],

time: 765 us -> 398 us (0.52)
  waiting for transfers between devices: 210 us -> 12.5 us
  Pallas kernels: 392 us -> 312 us
  blocking collectives: 70 us -> 0 us
  between operations: 14.9 us -> 1.57 us
    reduce_scatter x1 -> x0, waiting for transfers between devices: 140 us -> none  [per_device(): mine = lax.psum_scatter(partial, both, scatter_dimension=0, tiled=True)]
    pallas_call x1, Pallas kernels: 226 us -> 111 us  [per_device(): pl.pallas_call(functools.partial(backward_kernel, ntile=ntile, blocks=blo...]
    pallas_call x0 -> x3, Pallas kernels: none -> 94.4 us  [the longest x1 37.6 us: reduce_tiles(): pl.pallas_call(functools.partial(reduce_kernel, sizes=sizes), in_specs=[p...]
    all_gather x1 -> x0, blocking collectives: 70 us -> none  [per_device(): lax.all_gather(jnp.stack([own_tu, own_tv], axis=0), both, axis=1, tiled=T...]
    pallas_call x1, Pallas kernels: 166 us -> 106 us  [per_device(): pl.pallas_call(functools.partial(forward_kernel, ntile=ntile, blocks=bloc...]
    all_gather x1 -> x0, waiting for transfers between devices: 57.1 us -> none  [per_device(): lax.all_gather(contrib.reshape(sub_count, SUB // 2, LANES), both, tiled=T...]
    dynamic_slice x1 -> x0, local copies, waits for them, and re-layouts: 7.77 us -> none  [per_device(): lax.dynamic_slice_in_dim(model_image, (1 - core) * wide, wide, axis=2)]
  transfers between devices with their start and end apart: 4 -> 1, of which waited for: 3 -> 1; matrix products, arithmetic and copies ran while one was open for 2% -> 0% of each run, Pallas kernels for 0% -> 0%
where the time goes in v2:
time: 398 us; the launch traced here: 394 us
  Pallas kernels  312 us (78%)
  matrix products  29.2 us (7%)
  other arithmetic  20.9 us (5%)
  local copies, waits for them, and re-layouts  17.9 us (4%)
  waiting for transfers between devices  12.5 us (3%)
    pallas_call x1, Pallas kernels, per_device(): pl.pallas_call(functools.partial(backward_kernel, ntile=ntile, blocks=blo...  111 us
    pallas_call x1, Pallas kernels, per_device(): pl.pallas_call(functools.partial(forward_kernel, ntile=ntile, blocks=bloc...  106 us
    pallas_call x1, Pallas kernels, reduce_tiles(): pl.pallas_call(functools.partial(reduce_kernel, sizes=sizes), in_specs=[p...  37.6 us
    pallas_call x1, Pallas kernels, gather_tiles(): pl.pallas_call(functools.partial(gather_kernel, sizes=sizes), in_specs=[p...  34.3 us
    dot_general x24, matrix products, complex_einsum(): jnp.einsum(form, first, second, precision=lax.Precision.HIGH)  29.2 us
    pallas_call x1, Pallas kernels, swap_and_name(): pl.pallas_call(functools.partial(swap_kernel, bands=bands, groups=groups)...  22.5 us
    ppermute x1, waiting for transfers between devices, per_device(): arrived = lax.ppermute(leaving.reshape(2, rows, wide), 'slab', swap)  12.5 us
  transfers between devices with their start and end apart: 1, of which 1 were waited for; matrix products, arithmetic and copies ran while one was open for 0% of the time, Pallas kernels for 0%

profile of v2, /device:TPU:0, one launch (start us, length us, event | category | flops | bytes accessed | tf_op | source)
XLA Modules:
  0.0 394.1 jit_solution(4140561662416067414)
XLA Ops:
  0.7 1.0 sine_multiply_fusion.1
  1.7 1.7 fusion.96
  3.4 1.7 fusion.83
  5.1 1.7 fusion.82
  6.8 0.7 fusion.169
  7.5 0.6 pad.9.ids_ref
  8.1 0.1 fusion.145
  8.3 0.8 copy.46
  9.1 0.1 copy.47
  9.2 2.3 fusion.237
  11.5 22.5 %swap_columns.1 = (f32[2,8,256,512]{3,2,1,0:T(8,128)}, s32[32,8,128]{2,1,0:T(8,128)}) custom-call(s32[8,128]{1,0:T(8,128)} %pad.9.ids_ref, f32[2,8,256,1024]{3,2,1,0:T(8,128)} %bitcast.86), custom_call_target="tpu_custom_call" | custom-call | tf_op jit(solution)/shard_map/swap_columns/pallas_call | solution.py:561
  34.0 1.1 slice_reduce_fusion
  35.1 0.1 mul.521
  35.2 0.7 reshape_squeeze.3.tu_ref
  35.8 4.1 %fusion.19 = (f32[512,4,1,128]{3,0,2,1:T(8,128)S(1)}, f32[512,4,1,128]{3,0,2,1:T(8,128)S(1)}) fusion(s32[4,128]{1,0:T(4,128)S(1)} %add_add_fusion, s32[512]{0:T(512)S(1)} %mul.521), kind=kLoop, calls=%fused_computation.54 | loop fusion | flops 3670016 | bytes 2101248 | tf_op jit(solution)/shard_map/cos | solution.py:74
  40.0 0.1 pad_maximum_fusion
  40.2 3.0 copy.48
  43.2 0.7 pad.10.turn_ref
  43.8 0.2 fusion.16
  44.1 1.0 fusion.17.col_ref
  45.1 1.3 fusion.11
  46.3 1.7 pad_maximum_fusion.5
  48.0 105.9 %tiles_from_image.1 = f32[512,16,128]{2,1,0:T(8,128)} custom-call(s32[512]{0:T(512)} %reshape_squeeze.3.tu_ref, f32[2,8,256,1024]{3,2,1,0:T(8,128)} %bitcast.87, f32[2,8,256,512]{3,2,1,0:T(8,128)} %get-tuple-element.7.other_ref, bf16[512,1024]{1,0:T(8,128)(2,1)} %get-tuple-element.40.dft2_ref, bf16[512,512]{1,0:T(8,128)(2,1)} %get-tuple-element.15.dft1_ref, ...), custom_call_target="tpu_custom_call" | custom-call | tf_op jit(solution)/shard_map/tiles_from_image/pallas_call | solution.py:691
  153.9 37.6 %reduce_tiles.1 = f32[2,128,128]{2,1,0:T(8,128)} custom-call(f32[2,2,4,2,2,128,128]{6,5,4,3,2,1,0:T(8,128)} %bitcast.90), custom_call_target="tpu_custom_call" | custom-call | tf_op jit(solution)/shard_map/reduce_tiles/pallas_call | solution.py:591
  191.5 1.3 reshape_reshape.6
  192.9 0.1 copy.85
  193.0 0.4 fusion.140
  193.4 0.4 fusion.136
  193.8 0.4 fusion.7
  194.2 0.4 fusion.123
  194.6 0.4 fusion.138
  195.1 0.1 add_multiply_fusion
  195.2 0.4 fusion.6
  195.6 0.4 fusion.4
  196.0 0.4 fusion.5
  196.4 2.1 fusion.23
  198.6 2.1 fusion.21
  200.7 2.1 convolution_subtract_fusion.3
  202.8 3.4 fusion.52
  206.3 0.1 compare_select_fusion.1
  206.3 2.2 fusion.42
  208.5 2.1 fusion.20
  210.7 2.1 convolution_add_fusion.2
  212.8 2.2 convolution_subtract_fusion.2
  215.0 1.4 fusion.129
  216.4 1.4 fusion.133
  217.8 1.7 fusion.3
  219.5 0.4 fusion.118
  219.9 0.4 fusion.131
  220.3 1.4 fusion.2
  221.7 0.4 fusion.1
  222.1 0.4 fusion
  222.6 0.3 copy.67
  222.8 0.3 copy.66
  223.1 0.6 maximum_bitcast_fusion
  223.7 1.1 reshape_reshape.7.mine_ref
  224.8 34.3 %gather_tiles.1 = f32[2,2,4,2,2,128,128]{6,5,4,3,2,1,0:T(8,128)} custom-call(f32[2,128,128]{2,1,0:T(8,128)} %reshape_reshape.7.mine_ref), custom_call_target="tpu_custom_call" | custom-call | tf_op jit(solution)/shard_map/gather_tiles/pallas_call | solution.py:617
  259.1 1.0 reduce-precision_convert_fusion.3
  260.1 0.9 pad_maximum_fusion.7.col_ref
  261.0 111.3 %image_from_tiles.1 = (f32[2,8,256,1024]{3,2,1,0:T(8,128)}, f32[2,8,256,512]{3,2,1,0:T(8,128)}) custom-call(s32[512]{0:T(512)} %reshape_squeeze.3.tu_ref, f32[512,16,128]{2,1,0:T(8,128)} %bitcast.91, bf16[512,1024]{1,0:T(8,128)(2,1)} %get-tuple-element.41.dft2_ref, bf16[512,512]{1,0:T(8,128)(2,1)} %get-tuple-element.14.dft1_ref, f32[256,128]{1,0:T(8,128)} %pad.10.turn_ref, ...), custom_call_target="tpu_custom_call" | custom-call | tf_op jit(solution)/shard_map/image_from_tiles/pallas_call | solution.py:726
  372.3 0.5 collective-permute-start
  372.8 0.6 pad_maximum_fusion.9
  373.4 12.5 %collective-permute-done = f32[2,2048,512]{2,1,0:T(8,128)} collective-permute-done((f32[2,2048,512]{2,1,0:T(8,128)}, f32[2,2048,512]{2,1,0:T(8,128)}, u32[]{:S(2)}, u32[]{:S(2)}) %collective-permute-start) | collective-permute-done | bytes 8388640 | tf_op jit(solution)/shard_map/ppermute | solution.py:755
  385.9 7.8 %constant_dynamic-update-slice_fusion = f32[2,2048,1024]{2,1,0:T(8,128)} fusion(f32[2,2048,1024]{2,1,0:T(8,128)} %bitcast.122, f32[2,2048,512]{2,1,0:T(8,128)} %collective-permute-done, s32[]{:T(128)S(6)} %select_n.128), kind=kLoop, calls=%fused_computation.248 | loop fusion | bytes 16777220 | tf_op jit(solution)/shard_map/dynamic_update_slice | solution.py:756
  (36 shorter events, 0.3 us)
Async XLA Ops:
  40.0 3.2 copy-start.6
  40.0 3.9 copy-start
  40.0 3.9 copy-start.1
  40.0 3.8 copy-start.2
  40.2 4.9 %copy-start.3 = (f32[256,256]{1,0:T(8,128)S(1)}, f32[256,256]{1,0:T(8,128)}, u32[]{:S(2)}) copy-start(f32[256,256]{1,0:T(8,128)} %fusion.96) | copy-start | bytes 786436
  40.2 4.9 %copy-start.4 = (f32[256,256]{1,0:T(8,128)S(1)}, f32[256,256]{1,0:T(8,128)}, u32[]{:S(2)}) copy-start(f32[256,256]{1,0:T(8,128)} %fusion.83) | copy-start | bytes 786436
  40.2 4.9 %copy-start.5 = (f32[256,256]{1,0:T(8,128)S(1)}, f32[256,256]{1,0:T(8,128)}, u32[]{:S(2)}) copy-start(f32[256,256]{1,0:T(8,128)} %fusion.82) | copy-start | bytes 786436
  153.9 41.1 %copy-start.10 = (s32[16]{0:T(128)S(1)}, s32[16]{0:T(128)}, u32[]{:S(2)}) copy-start(s32[16]{0:T(128)} %param.12) | copy-start | bytes 196
  153.9 41.2 %copy-start.8 = (f32[16,2,128]{2,1,0:T(2,128)S(1)}, f32[16,2,128]{2,1,0:T(2,128)}, u32[]{:S(2)}) copy-start(f32[16,2,128]{2,1,0:T(2,128)} %param.8) | copy-start | bytes 49156
  193.8 12.4 %copy-start.7 = (f32[16,2,128]{2,1,0:T(2,128)S(1)}, f32[16,2,128]{2,1,0:T(2,128)}, u32[]{:S(2)}) copy-start(f32[16,2,128]{2,1,0:T(2,128)} %param.9) | copy-start | bytes 49156
  193.8 12.4 %copy-start.9 = (s32[16]{0:T(128)S(1)}, s32[16]{0:T(128)}, u32[]{:S(2)}) copy-start(s32[16]{0:T(128)} %param.13) | copy-start | bytes 196
  372.3 13.6 %collective-permute-start = (f32[2,2048,512]{2,1,0:T(8,128)}, f32[2,2048,512]{2,1,0:T(8,128)}, u32[]{:S(2)}, u32[]{:S(2)}) collective-permute-start(f32[2,2048,512]{2,1,0:T(8,128)} %bitcast.123), channel_id=1, source_target_pairs={{0,8},{8,0},{16,24},{24,16},{1,9},{9,1},{17,25},{25,17},{2,10},{10... | collective-permute-start | bytes 25165832 | tf_op jit(solution)/shard_map/ppermute | solution.py:755

commit v3 on v2

--- a/solution.py
+++ b/solution.py
@@ -17,11 +17,13 @@
 
 
 def complex_einsum(form, left, right):
-    product = lambda first, second: jnp.einsum(form, first, second, precision=lax.Precision.HIGH)
-    return (
-        product(left[0], right[0]) - product(left[1], right[1]),
-        product(left[0], right[1]) + product(left[1], right[0]),
-    )
+    names, made = form.split("->")
+    first, second = names.split(",")
+    re, im = right
+    table = jnp.stack([jnp.stack([re, im]), jnp.stack([-im, re])])
+    out = jnp.einsum(
+        f"P{first},PQ{second}->Q{made}", jnp.stack(left), table, precision=lax.Precision.HIGH)
+    return out[0], out[1]
 
 
 def complex_mul(left, right):

time: 398 us -> 380 us (0.955)
  matrix products: 29.2 us -> 3.15 us
  other arithmetic: 20.9 us -> 31.2 us
    dot_general x24 -> x6, matrix products: 29.2 us -> 3.15 us  [complex_einsum(): jnp.einsum(f'P{first},PQ{second}->Q{made}', jnp.stack(left), table, preci...]
where the time goes in v3:
time: 380 us; the launch traced here: 378 us
  Pallas kernels  312 us (82%)
  other arithmetic  31.2 us (8%)
  local copies, waits for them, and re-layouts  18.3 us (5%)
  waiting for transfers between devices  12.5 us (3%)
    pallas_call x1, Pallas kernels, per_device(): pl.pallas_call(functools.partial(backward_kernel, ntile=ntile, blocks=blo...  111 us
    pallas_call x1, Pallas kernels, per_device(): pl.pallas_call(functools.partial(forward_kernel, ntile=ntile, blocks=bloc...  106 us
    pallas_call x1, Pallas kernels, reduce_tiles(): pl.pallas_call(functools.partial(reduce_kernel, sizes=sizes), in_specs=[p...  37.6 us
    pallas_call x1, Pallas kernels, gather_tiles(): pl.pallas_call(functools.partial(gather_kernel, sizes=sizes), in_specs=[p...  34.3 us
    pallas_call x1, Pallas kernels, swap_and_name(): pl.pallas_call(functools.partial(swap_kernel, bands=bands, groups=groups)...  22.5 us
    ppermute x1, waiting for transfers between devices, per_device(): arrived = lax.ppermute(leaving.reshape(2, rows, wide), 'slab', swap)  12.5 us
    dynamic_update_slice x1, local copies, waits for them, and re-layouts, per_device(): lax.dynamic_update_slice_in_dim(image.reshape(2, rows, cols), arrived, (1...  7.76 us
  transfers between devices with their start and end apart: 1, of which 1 were waited for; matrix products, arithmetic and copies ran while one was open for 0% of the time, Pallas kernels for 0%

profile of v3, /device:TPU:0, one launch (start us, length us, event | category | flops | bytes accessed | tf_op | source)
XLA Modules:
  0.0 378.4 jit_solution(3914163230475460969)
XLA Ops:
  0.6 0.5 fusion.105
  1.2 0.6 add_add_fusion
  1.8 1.0 sine_multiply_fusion.1
  2.8 1.7 fusion.64
  4.5 1.7 fusion.63
  6.2 1.7 fusion.62
  7.9 1.2 convert_multiply_fusion
  9.0 0.7 fusion.103
  9.7 0.6 pad.9.ids_ref
  10.3 0.1 add_multiply_fusion
  10.4 1.4 slice_multiply_fusion.4
  11.8 0.7 fusion.102
  12.5 0.1 fusion.96
  12.7 0.1 copy.31
  12.8 0.8 copy.32
  13.5 0.1 copy.33
  13.7 2.0 fusion.111
  15.6 22.5 %swap_columns.1 = (f32[2,8,256,512]{3,2,1,0:T(8,128)}, s32[32,8,128]{2,1,0:T(8,128)}) custom-call(s32[8,128]{1,0:T(8,128)} %pad.9.ids_ref, f32[2,8,256,1024]{3,2,1,0:T(8,128)} %bitcast.127), custom_call_target="tpu_custom_call" | custom-call | tf_op jit(solution)/shard_map/swap_columns/pallas_call | solution.py:563
  38.1 1.1 slice_reduce_fusion
  39.2 0.1 mul.615
  39.3 0.6 reshape_squeeze.3.tu_ref
  39.9 4.8 %fusion.26 = (f32[512,4,1,128]{3,0,2,1:T(8,128)S(1)}, f32[512,4,1,128]{3,0,2,1:T(8,128)S(1)}) fusion(s32[4,128]{1,0:T(4,128)} %add_add_fusion, s32[512]{0:T(512)S(1)} %mul.615), kind=kLoop, calls=%fused_computation.67 | loop fusion | flops 3670016 | bytes 2101248 | tf_op jit(solution)/shard_map/cos | solution.py:76
  44.7 0.1 pad_maximum_fusion
  44.9 0.0 copy-start.4
  44.9 2.9 copy.34
  47.9 0.7 pad.10.turn_ref
  48.5 0.2 fusion.21
  48.7 1.0 fusion.22.col_ref
  49.7 1.2 fusion.3
  51.0 1.7 pad_maximum_fusion.5
  52.6 105.9 %tiles_from_image.1 = f32[512,16,128]{2,1,0:T(8,128)} custom-call(s32[512]{0:T(512)} %reshape_squeeze.3.tu_ref, f32[2,8,256,1024]{3,2,1,0:T(8,128)} %bitcast.128, f32[2,8,256,512]{3,2,1,0:T(8,128)} %get-tuple-element.7.other_ref, bf16[512,1024]{1,0:T(8,128)(2,1)} %get-tuple-element.71.dft2_ref, bf16[512,512]{1,0:T(8,128)(2,1)} %get-tuple-element.17.dft1_ref, ...), custom_call_target="tpu_custom_call" | custom-call | tf_op jit(solution)/shard_map/tiles_from_image/pallas_call | solution.py:693
  158.5 37.6 %reduce_tiles.1 = f32[2,128,128]{2,1,0:T(8,128)} custom-call(f32[2,2,4,2,2,128,128]{6,5,4,3,2,1,0:T(8,128)} %bitcast.131), custom_call_target="tpu_custom_call" | custom-call | tf_op jit(solution)/shard_map/reduce_tiles/pallas_call | solution.py:593
  196.2 1.4 reshape_reshape.6
  197.5 0.1 copy.96
  197.6 0.1 copy.37
  197.8 0.1 copy.36
  198.0 1.0 fusion.65
  199.0 0.1 maximum_bitcast_fusion
  199.2 0.6 convolution_bitcast_fusion.4
  199.8 0.0 copy-start.17
  199.8 0.4 convolution_bitcast_fusion.2
  200.2 0.3 fusion.20
  200.5 1.2 fusion.50
  201.7 0.6 convolution_bitcast_fusion.1
  202.3 1.2 fusion.45
  203.5 0.1 compare_select_fusion.1
  203.7 1.0 fusion.48
  204.7 0.6 fusion.7
  205.3 1.2 fusion.112
  206.5 0.1 maximum_bitcast_fusion.4
  206.6 0.6 convolution_bitcast_fusion.3
  207.2 0.4 convolution_bitcast_fusion
  207.7 0.1 copy.48
  207.9 0.1 copy.49
  208.0 0.4 copy.50
  208.5 1.1 reshape_reshape.7.mine_ref
  209.5 34.3 %gather_tiles.1 = f32[2,2,4,2,2,128,128]{6,5,4,3,2,1,0:T(8,128)} custom-call(f32[2,128,128]{2,1,0:T(8,128)} %reshape_reshape.7.mine_ref), custom_call_target="tpu_custom_call" | custom-call | tf_op jit(solution)/shard_map/gather_tiles/pallas_call | solution.py:619
  243.8 1.0 reduce-precision_convert_fusion.3
  244.8 0.9 pad_maximum_fusion.13.col_ref
  245.7 111.4 %image_from_tiles.1 = (f32[2,8,256,1024]{3,2,1,0:T(8,128)}, f32[2,8,256,512]{3,2,1,0:T(8,128)}) custom-call(s32[512]{0:T(512)} %reshape_squeeze.3.tu_ref, f32[512,16,128]{2,1,0:T(8,128)} %bitcast.132, bf16[512,1024]{1,0:T(8,128)(2,1)} %get-tuple-element.72.dft2_ref, bf16[512,512]{1,0:T(8,128)(2,1)} %get-tuple-element.16.dft1_ref, f32[256,128]{1,0:T(8,128)} %pad.10.turn_ref, ...), custom_call_target="tpu_custom_call" | custom-call | tf_op jit(solution)/shard_map/image_from_tiles/pallas_call | solution.py:728
  357.1 0.4 collective-permute-start
  357.6 0.6 pad_maximum_fusion.21
  358.2 12.5 %collective-permute-done = f32[2,2048,512]{2,1,0:T(8,128)} collective-permute-done((f32[2,2048,512]{2,1,0:T(8,128)}, f32[2,2048,512]{2,1,0:T(8,128)}, u32[]{:S(2)}, u32[]{:S(2)}) %collective-permute-start) | collective-permute-done | bytes 8388640 | tf_op jit(solution)/shard_map/ppermute | solution.py:757
  370.7 7.8 %constant_dynamic-update-slice_fusion = f32[2,2048,1024]{2,1,0:T(8,128)} fusion(f32[2,2048,1024]{2,1,0:T(8,128)} %bitcast.146, f32[2,2048,512]{2,1,0:T(8,128)} %collective-permute-done, s32[]{:T(128)S(6)} %select_n.128), kind=kLoop, calls=%fused_computation.209 | loop fusion | bytes 16777220 | tf_op jit(solution)/shard_map/dynamic_update_slice | solution.py:758
  (49 shorter events, 0.4 us)
Async XLA Ops:
  44.7 3.2 copy-start.6
  44.7 3.8 %copy-start = (f32[512,32]{1,0:T(8,128)S(1)}, f32[512,32]{1,0:T(8,128)}, u32[]{:S(2)}) copy-start(f32[512,32]{1,0:T(8,128)} %get-tuple-element.37) | copy-start | bytes 196612
  44.7 3.8 %copy-start.1 = (f32[512,32]{1,0:T(8,128)S(1)}, f32[512,32]{1,0:T(8,128)}, u32[]{:S(2)}) copy-start(f32[512,32]{1,0:T(8,128)} %get-tuple-element.38) | copy-start | bytes 196612
  44.7 3.8 %copy-start.2 = (f32[512,32]{1,0:T(8,128)S(1)}, f32[512,32]{1,0:T(8,128)}, u32[]{:S(2)}) copy-start(f32[512,32]{1,0:T(8,128)} %get-tuple-element.39) | copy-start | bytes 196612
  44.9 4.8 %copy-start.3 = (f32[256,256]{1,0:T(8,128)S(1)}, f32[256,256]{1,0:T(8,128)}, u32[]{:S(2)}) copy-start(f32[256,256]{1,0:T(8,128)} %fusion.64) | copy-start | bytes 786436
  44.9 4.8 %copy-start.4 = (f32[256,256]{1,0:T(8,128)S(1)}, f32[256,256]{1,0:T(8,128)}, u32[]{:S(2)}) copy-start(f32[256,256]{1,0:T(8,128)} %fusion.63) | copy-start | bytes 786436
  44.9 4.8 %copy-start.5 = (f32[256,256]{1,0:T(8,128)S(1)}, f32[256,256]{1,0:T(8,128)}, u32[]{:S(2)}) copy-start(f32[256,256]{1,0:T(8,128)} %fusion.62) | copy-start | bytes 786436
  196.1 1.8 copy-start.13
  196.1 1.8 copy-start.15
  196.2 3.0 copy-start.7
  196.2 3.0 copy-start.8
  198.0 2.5 copy-start.16
  199.8 3.8 copy-start.14
  199.8 3.8 copy-start.17
  203.6 3.6 copy-start.9
  203.6 3.6 copy-start.11
  245.7 111.9 %copy-start.10 = (f32[16,1,128]{2,1,0:T(1,128)S(1)}, f32[16,1,128]{2,1,0:T(1,128)}, u32[]{:S(2)}) copy-start(f32[16,1,128]{2,1,0:T(1,128)} %copy-done.9) | copy-start | bytes 24580
  245.7 111.9 %copy-start.12 = (f32[16,1,128]{2,1,0:T(1,128)S(1)}, f32[16,1,128]{2,1,0:T(1,128)}, u32[]{:S(2)}) copy-start(f32[16,1,128]{2,1,0:T(1,128)} %copy-done.11) | copy-start | bytes 24580
  357.1 13.6 %collective-permute-start = (f32[2,2048,512]{2,1,0:T(8,128)}, f32[2,2048,512]{2,1,0:T(8,128)}, u32[]{:S(2)}, u32[]{:S(2)}) collective-permute-start(f32[2,2048,512]{2,1,0:T(8,128)} %bitcast.147), channel_id=1, source_target_pairs={{0,8},{8,0},{16,24},{24,16},{1,9},{9,1},{17,25},{25,17},{2,10},{10... | collective-permute-start | bytes 25165832 | tf_op jit(solution)/shard_map/ppermute | solution.py:757
